TPU v7x, 8 devices: a whole 2x2x1 slice. The times are simulated.
8 devices in a mesh: rep: 1 (over z), dp: 2 (over y), sp: 4 (over x, core).
Axes of the slice: x: 2, y: 2, z: 1, core: 2. Of those that a mesh axis runs over, the one named last changes fastest.
Arguments:
- hidden: bfloat16 [128, 2048], P(('rep', 'dp'))
- w_query: bfloat16 [2048, 2048], replicated
- w_key: bfloat16 [2048, 256], replicated
- w_value: bfloat16 [2048, 256], replicated
- w_out: bfloat16 [2048, 2048], P('sp')
- k_cache: bfloat16 [128, 2048, 1, 256], P(('rep', 'dp'), 'sp')
- v_cache: bfloat16 [128, 2048, 1, 256], P(('rep', 'dp'), 'sp')
- write_pos: int32 [128], P(('rep', 'dp'))
- valid_len: int32 [128], P(('rep', 'dp'))
Outputs:
- output 1: bfloat16 [128, 2048], P(('rep', 'dp'))
- output 2: bfloat16 [128, 2048, 1, 256], P(('rep', 'dp'), 'sp')
- output 3: bfloat16 [128, 2048, 1, 256], P(('rep', 'dp'), 'sp')
All inputs are finite; a program needn't handle non-finite values.
Results may differ from a plain program's by a relative error of at most 0.00615348.
Values are sent between devices in bfloat16 or wider.
A program may use at most 1 GiB of HBM per device.

v0:
```python
import jax
import jax.numpy as jnp
from jax import lax
from jax.sharding import PartitionSpec as P

NEG_FLOOR = -1e30


def solution(mesh):
    row_spec = P(('rep', 'dp'), None)
    cache_spec = P(('rep', 'dp'), 'sp', None, None)
    len_spec = P(('rep', 'dp'))

    def local_step(hidden, w_query, w_key, w_value, w_out, k_cache, v_cache, write_pos, valid_len):
        num_rows, seq_local, kv_heads, head_dim = k_cache.shape
        num_heads = w_query.shape[1] // head_dim
        group_size = num_heads // kv_heads
        shard_idx = lax.axis_index('sp')
        query = jnp.dot(hidden, w_query, preferred_element_type=jnp.float32).astype(jnp.bfloat16)
        query = query.reshape(num_rows, kv_heads, group_size, head_dim)
        key_new = jnp.dot(hidden, w_key, preferred_element_type=jnp.float32).astype(jnp.bfloat16)
        value_new = jnp.dot(hidden, w_value, preferred_element_type=jnp.float32).astype(jnp.bfloat16)
        positions = shard_idx * seq_local + jnp.arange(seq_local, dtype=jnp.int32)
        at_pos = (positions[None, :] == write_pos[:, None])[:, :, None, None]
        k_next = jnp.where(at_pos, key_new.reshape(num_rows, 1, kv_heads, head_dim), k_cache)
        v_next = jnp.where(at_pos, value_new.reshape(num_rows, 1, kv_heads, head_dim), v_cache)
        scores = jnp.einsum('bkgd,bskd->bkgs', query, k_next, preferred_element_type=jnp.float32) * head_dim ** -0.5
        valid_mask = (positions[None, :] < valid_len[:, None])[:, None, None, :]
        scores = jnp.where(valid_mask, scores, -jnp.inf)
        local_max = jnp.maximum(jnp.max(scores, axis=-1), NEG_FLOOR)
        weights = jnp.exp(scores - local_max[..., None])
        local_sum = jnp.sum(weights, axis=-1)
        local_acc = jnp.einsum('bkgs,bskd->bkgd', weights.astype(jnp.bfloat16), v_next, preferred_element_type=jnp.float32)
        global_max = lax.pmax(local_max, 'sp')
        rescale = jnp.exp(local_max - global_max)
        packed = jnp.concatenate([local_acc * rescale[..., None], (local_sum * rescale)[..., None]], axis=-1)
        packed = lax.psum(packed, 'sp')
        attention = (packed[..., :head_dim] / packed[..., head_dim:]).astype(jnp.bfloat16)
        attention = attention.reshape(num_rows, num_heads * head_dim)
        out_rows = w_out.shape[0]
        attn_mine = lax.dynamic_slice_in_dim(attention, shard_idx * out_rows, out_rows, axis=1)
        partial_out = jnp.dot(attn_mine, w_out, preferred_element_type=jnp.float32)
        attn_out = lax.psum(partial_out, 'sp').astype(jnp.bfloat16)
        return attn_out, k_next, v_next

    return jax.shard_map(local_step, mesh=mesh, in_specs=(row_spec, P(), P(), P(), P('sp', None), cache_spec, cache_spec, len_spec, len_spec), out_specs=(row_spec, cache_spec, cache_spec), check_vma=False)
```

profile of v0, /device:TPU:0, one launch (start us, length us, event | category | flops | bytes accessed | tf_op | source)
XLA Modules:
  0.0 128.7 jit_solution(16821136088838985791)
XLA Ops:
  7.2 0.0 copy-start
  7.2 0.0 all-reduce.3.cloned.1.call-start
  7.3 1.7 %convolution_convert_fusion.2 = bf16[64,256]{1,0:T(8,128)(2,1)S(1)} fusion(bf16[64,2048]{1,0:T(8,128)(2,1)} %param.9, bf16[2048,256]{1,0:T(8,128)(2,1)} %param.11), kind=kOutput, calls=%fused_computation.12 | convolution fusion | flops 67125248 | bytes 1343488 | tf_op jit(solution)/shard_map/dot_general | solution.py:21
  9.0 1.6 %convolution_convert_fusion.1 = bf16[64,256]{1,0:T(8,128)(2,1)S(1)} fusion(bf16[64,2048]{1,0:T(8,128)(2,1)} %param.9, bf16[2048,256]{1,0:T(8,128)(2,1)} %param.12), kind=kOutput, calls=%fused_computation.11 | convolution fusion | flops 67125248 | bytes 1343488 | tf_op jit(solution)/shard_map/dot_general | solution.py:22
  10.6 5.0 %convolution_convert_fusion = bf16[64,2048]{1,0:T(8,128)(2,1)S(1)} fusion(bf16[64,2048]{1,0:T(8,128)(2,1)} %param.9, bf16[2048,2048]{1,0:T(8,128)(2,1)} %param.10), kind=kOutput, calls=%fused_computation.6 | convolution fusion | flops 537001984 | bytes 8912896 | tf_op jit(solution)/shard_map/dot_general | solution.py:19
  15.7 0.1 copy.24
  15.7 0.0 copy-done.1
  15.7 0.0 copy-done.2
  15.7 0.1 broadcast_compare_fusion.1
  15.9 23.1 %broadcast_select_fusion = (bf16[64,512,1,256]{3,1,2,0:T(8,128)(2,1)}, bf16[64,512,1,256]{3,1,2,0:T(8,128)(2,1)}) fusion(bf16[64,512,1,256]{3,1,2,0:T(8,128)(2,1)} %param.15, pred[64,512]{1,0:T(8,128)(4,1)S(1)} %get-tuple-element.10, bf16[64,256]{1,0:T(8,128)(2,1)S(1)} %convolution_convert_fusion.1, bf16[64,512,1,256]{3,1,2,0:T(8,128)(2,1)} %param.14, ...), kind=kLoop, calls=%fused_computation.4 | loop fusion | flops 16777216 | bytes 67207168 | tf_op jit(solution)/shard_map/jit(_where)/select_n | solution.py:26
  38.9 10.3 %fusion.27 = (f32[64,8]{1,0:T(8,128)S(1)}, f32[64,8,512]{2,1,0:T(8,128)S(1)}) fusion(bf16[64,8,256]{2,1,0:T(8,128)(2,1)S(1)} %bitcast.46, bf16[64,512,1,256]{3,1,2,0:T(8,128)(2,1)} %get-tuple-element.6, pred[64,512]{1,0:T(8,128)(4,1)S(1)} %get-tuple-element.9), kind=kOutput, calls=%fused_computation.32 | convolution fusion | flops 135003648 | bytes 18122752 | tf_op jit(solution)/shard_map/bkgd,bskd->bkgs/dot_general | solution.py:27
  49.2 13.3 %pmax.7 = f32[64,1,8]{2,0,1:T(8,128)S(1)} all-reduce(f32[64,1,8]{2,0,1:T(8,128)S(1)} %get-tuple-element.7), channel_id=1, replica_groups=mesh['rep'=1,'dp'=2,'sp'=4] {'sp'}, use_global_device_ids=true, to_apply=%region_1.2 | all-reduce | flops 512 | bytes 4096 | tf_op jit(solution)/shard_map/pmax | solution.py:34
  62.5 0.3 fusion.16
  62.8 0.4 copy.18
  63.3 8.1 %fusion.13 = f32[64,1,8,256]{3,2,0,1:T(8,128)S(1)} fusion(bf16[64,512,1,256]{3,1,2,0:T(8,128)(2,1)} %get-tuple-element.5, f32[64,8,512]{2,1,0:T(8,128)S(1)} %get-tuple-element.12, f32[64,8]{1,0:T(8,128)S(1)} %get-tuple-element.8, f32[64,8]{1,0:T(8,128)S(1)} %get-tuple-element.3), kind=kOutput, calls=%fused_computation.10 | convolution fusion | flops 134873088 | bytes 18354176 | tf_op jit(solution)/shard_map/bkgs,bskd->bkgd/dot_general | solution.py:33
  71.4 1.0 pad_maximum_fusion
  72.4 0.0 all-reduce.3.cloned.1.call-update
  72.4 29.6 %all-reduce.3.cloned.1.call-done = f32[64,1,8,257]{3,2,0,1:T(8,128)} async-done(((f32[64,1,8,257]{3,2,0,1:T(8,128)}), f32[64,1,8,257]{3,2,0,1:T(8,128)}) %all-reduce.3.cloned.1.call-update) | async-done | bytes 526352 | tf_op jit(solution)/shard_map/psum | solution.py:37
  102.0 1.0 slice.9
  103.0 0.4 copy.23
  103.4 1.2 fusion.19
  104.6 0.1 copy.25
  104.7 0.5 fusion.21
  105.2 16.7 %all-reduce.4 = bf16[64,2048]{1,0:T(8,128)(2,1)} all-reduce(f32[64,2048]{1,0:T(8,128)S(1)} %fusion.21), channel_id=1, replica_groups=mesh['rep'=1,'dp'=2,'sp'=4] {'sp'}, use_global_device_ids=true, to_apply=%region_4.5 | all-reduce | flops 131072 | bytes 786432 | tf_op jit(solution)/shard_map/psum | solution.py:43
  (6 shorter events, 0.0 us)
Async XLA Ops:
  7.2 97.5 %copy-start = (bf16[512,2048]{1,0:T(8,128)(2,1)S(1)}, bf16[512,2048]{1,0:T(8,128)(2,1)}, u32[]{:S(2)}) copy-start(bf16[512,2048]{1,0:T(8,128)(2,1)} %param.13) | copy-start | bytes 6291460
  7.2 8.5 %copy-start.1 = (s32[64]{0:T(128)S(1)}, s32[64]{0:T(128)}, u32[]{:S(2)}) copy-start(s32[64]{0:T(128)} %param.17) | copy-start | bytes 772
  7.2 8.5 %copy-start.2 = (s32[64]{0:T(128)S(1)}, s32[64]{0:T(128)}, u32[]{:S(2)}) copy-start(s32[64]{0:T(128)} %param.16) | copy-start | bytes 772
  7.2 94.8 %all-reduce.3.cloned.1.call-start = ((), (), s32[]{:S(2)}) async-start(), calls=%async_computation | async-start | bytes 1572864 | tf_op jit(solution)/shard_map/psum | solution.py:37
Sparse Core Ops, SparseCore 0:
  72.5 29.4 all-reduce.2
where the time goes:
time: 129 us
  blocking collectives  30 us (23%)
  waiting for transfers between devices  29.6 us (23%)
  matrix products  27.2 us (21%)
  other arithmetic  25.7 us (20%)
  between operations  14.2 us (11%)
  local copies, waits for them, and re-layouts  1.97 us (2%)
    psum x1, waiting for transfers between devices, local_step(): packed = lax.psum(packed, 'sp')  29.6 us
    select_n x1, other arithmetic, local_step(): jnp.where(at_pos, value_new.reshape(num_rows, 1, kv_heads, head_dim), v_c...  23.1 us
    psum x1, blocking collectives, local_step(): attn_out = lax.psum(partial_out, 'sp').astype(jnp.bfloat16)  16.7 us
    pmax x1, blocking collectives, local_step(): global_max = lax.pmax(local_max, 'sp')  13.3 us
    dot_general x1, matrix products, local_step(): jnp.einsum('bkgd,bskd->bkgs', query, k_next, preferred_element_type=jnp.f...  10.3 us
    dot_general x1, matrix products, local_step(): jnp.einsum('bkgs,bskd->bkgd', weights.astype(jnp.bfloat16), v_next, prefe...  8.09 us
    dot_general x1, matrix products, local_step(): jnp.dot(hidden, w_query, preferred_element_type=jnp.float32)  5.05 us
  transfers between devices with their start and end apart: 1, of which 1 were waited for; matrix products, arithmetic and copies ran while one was open for 0% of the time, Pallas kernels for 0%

commit v1 on v0

v1 whole, which is shorter than its diff:
```python
import functools

import jax
import jax.numpy as jnp
from jax import lax
from jax.experimental import pallas as pl
from jax.experimental.pallas import tpu as pltpu
from jax.sharding import PartitionSpec as P

F32, BF16 = jnp.float32, jnp.bfloat16
NEG_FLOOR = -1e30
GROUP = 8
AHEAD = 3
ANY = pl.BlockSpec(memory_space=pl.ANY)
VMEM = pl.BlockSpec(memory_space=pltpu.VMEM)


def attend(hid_hbm, wq_hbm, wk_hbm, wv_hbm, k_hbm, v_hbm, pos_hbm, len_hbm,
           acc_ref, ml_ref, k_out, v_out,
           hid, wq, wk, wv, q_all, k_row, v_row, pos, length, sem_w, sem_s, sem_k, sem_v):
    rows, span, dim = k_out.shape
    heads = q_all.shape[0]
    groups = rows // GROUP
    start = lax.axis_index('sp') * span

    def fetch(g):
        part = pl.ds(g * GROUP, GROUP)
        return (pltpu.make_async_copy(k_hbm.at[part], k_out.at[part], sem_k.at[g]),
                pltpu.make_async_copy(v_hbm.at[part], v_out.at[part], sem_v.at[g]))

    def q_part(h):
        cols = pl.ds(h * dim, dim)
        return pltpu.make_async_copy(wq_hbm.at[:, cols], wq.at[:, cols], sem_w.at[3 + h])

    scal = [pltpu.make_async_copy(pos_hbm, pos, sem_s.at[0]), pltpu.make_async_copy(len_hbm, length, sem_s.at[1])]
    first = [pltpu.make_async_copy(hid_hbm, hid, sem_w.at[0]),
             pltpu.make_async_copy(wk_hbm, wk, sem_w.at[1]),
             pltpu.make_async_copy(wv_hbm, wv, sem_w.at[2])]
    for c in scal + first + [q_part(h) for h in range(heads)]:
        c.start()
    for g in range(AHEAD):
        for c in fetch(g):
            c.start()
    for c in scal:
        c.wait()
    first[0].wait()
    first[1].wait()
    k_row[...] = jnp.dot(hid[...], wk[...], preferred_element_type=F32).astype(BF16).astype(F32)
    first[2].wait()
    v_row[...] = jnp.dot(hid[...], wv[...], preferred_element_type=F32).astype(BF16).astype(F32)
    for h in range(heads):
        q_part(h).wait()
        q_all[h] = jnp.dot(hid[...], wq[:, h * dim:(h + 1) * dim], preferred_element_type=F32).astype(BF16).astype(F32)

    def step(g, ml):
        for c in fetch(g):
            c.wait()

        @pl.when(g + AHEAD < groups)
        def _():
            for c in fetch(g + AHEAD):
                c.start()

        base = g * GROUP
        q = jnp.swapaxes(q_all[:, pl.ds(pl.multiple_of(base, GROUP), GROUP), :], 0, 1)
        sub = lax.broadcasted_iota(jnp.int32, (16, dim), 0)
        for j in range(GROUP):
            at = pos[base + j] - start
            inside = jnp.logical_and(at >= 0, at < span)
            at = jnp.where(inside, at, 0)
            win = pl.ds(pl.multiple_of(at // 16 * 16, 16), 16)
            hit = jnp.logical_and(sub == at % 16, inside)
            for row, buf in ((k_row, k_out), (v_row, v_out)):
                new = row[pl.ds(base + j, 1), :]
                old = buf[base + j, win, :].astype(F32)
                buf[base + j, win, :] = jnp.where(hit, new, old).astype(BF16)
        col = lax.broadcasted_iota(jnp.int32, (heads, span), 1)
        lane = lax.broadcasted_iota(jnp.int32, ml.shape, 1)
        scores = []
        for j in range(GROUP):
            s = lax.dot_general(q[j].astype(BF16), k_out[base + j], (((1,), (1,)), ((), ())), preferred_element_type=F32)
            scores.append(jnp.where(col < length[base + j] - start, s * dim ** -0.5, -jnp.inf))
        probs = []
        for j in range(GROUP):
            m = jnp.maximum(jnp.max(scores[j], axis=1, keepdims=True), NEG_FLOOR)
            p = jnp.exp(scores[j] - m)
            ml = jnp.where(lane == base + j, m, ml)
            ml = jnp.where(lane == rows + base + j, jnp.sum(p, axis=1, keepdims=True), ml)
            probs.append(p.astype(BF16))
        out = [jnp.dot(probs[j], v_out[base + j], preferred_element_type=F32) for j in range(GROUP)]
        acc_ref[:, pl.ds(pl.multiple_of(base, GROUP), GROUP), :] = jnp.swapaxes(jnp.stack(out), 0, 1)
        return ml

    ml_ref[...] = lax.fori_loop(0, groups, step, jnp.zeros(ml_ref.shape, F32))


def finish(acc, ml, wo_hbm, out, wo, ml_in, part1, send2, part2, mine, half, part3, send4, part4, done, part5,
           sem_w, send, recv):
    i = lax.axis_index('sp')
    x, c = i // 2, i % 2
    pair, across, far = 2 * x + 1 - c, 2 * (1 - x) + c, 2 * (1 - x) + 1 - c
    rows = acc.shape[1]
    wide = half.shape[2]
    barrier = pltpu.get_barrier_semaphore()
    for peer in (pair, across, far):
        pl.semaphore_signal(barrier, inc=1, device_id={'sp': peer}, device_id_type=pl.DeviceIdType.MESH)
    load = pltpu.make_async_copy(wo_hbm, wo, sem_w)
    load.start()
    pl.semaphore_wait(barrier, 3)

    def to(n, src, dst, peer):
        return pltpu.make_async_remote_copy(src_ref=src, dst_ref=dst, send_sem=send.at[n], recv_sem=recv.at[n],
                                            device_id={'sp': peer}, device_id_type=pl.DeviceIdType.MESH)

    def heads_of(xx, cc):
        return 4 * xx + 2 * cc

    c_ml = [to(n, ml, ml_in.at[n], peer) for n, peer in enumerate((pair, across, far))]
    c_1 = [to(3, acc.at[pl.ds(heads_of(1 - x, 1 - c), 2)], part1.at[0], pair),
           to(4, acc.at[pl.ds(heads_of(x, 1 - c), 2)], part1.at[1], pair)]
    for copy in c_ml + c_1:
        copy.start()

    def split(v):
        t = v.T
        return t[:rows], t[rows:]

    lane = lax.broadcasted_iota(jnp.int32, (rows, ml.shape[0]), 1)

    def col(v, h):
        return jnp.sum(jnp.where(lane == h, v, 0.0), axis=1, keepdims=True)

    m0, l0 = split(ml[...])
    c_ml[0].wait()
    m1, l1 = split(ml_in[0])
    mp = jnp.maximum(m0, m1)
    e0, e1 = jnp.exp(m0 - mp), jnp.exp(m1 - mp)
    lp = l0 * e0 + l1 * e1
    c_1[0].wait()
    for j in range(2):
        h = heads_of(1 - x, c) + j
        send2[j] = acc[h] * col(e0, h) + part1[0, j] * col(e1, h)
    c_2 = to(5, send2, part2, across)
    c_2.start()
    c_1[1].wait()
    for j in range(2):
        h = heads_of(x, c) + j
        mine[j] = acc[h] * col(e0, h) + part1[1, j] * col(e1, h)
    c_ml[1].wait()
    c_ml[2].wait()
    m2, l2 = split(ml_in[1])
    m3, l3 = split(ml_in[2])
    mq = jnp.maximum(m2, m3)
    lq = l2 * jnp.exp(m2 - mq) + l3 * jnp.exp(m3 - mq)
    mt = jnp.maximum(mp, mq)
    ep, eq = jnp.exp(mp - mt), jnp.exp(mq - mt)
    inv = 1.0 / (lp * ep + lq * eq)
    ep, eq = ep * inv, eq * inv
    factors = [(col(ep, heads_of(x, c) + j), col(eq, heads_of(x, c) + j)) for j in range(2)]
    load.wait()
    c_2.wait()
    o = jnp.concatenate([(mine[j] * factors[j][0] + part2[j] * factors[j][1]).astype(BF16) for j in range(2)], axis=1)

    def project(side):
        cols = pl.ds(pl.multiple_of(side * wide, wide), wide)
        return jnp.dot(o, wo[:, cols], preferred_element_type=F32)

    half[0] = project(1 - c)
    c_3 = to(6, half.at[0], part3, pair)
    c_3.start()
    half[1] = project(c)
    c_3.wait()
    send4[...] = half[1] + part3[...]
    c_4 = to(7, send4, part4, across)
    c_4.start()
    c_4.wait()
    done[...] = (send4[...] + part4[...]).astype(BF16)
    c_5 = to(8, done, part5, pair)
    c_5.start()
    out[:, pl.ds(pl.multiple_of(c * wide, wide), wide)] = done[...]
    c_5.wait()
    out[:, pl.ds(pl.multiple_of((1 - c) * wide, wide), wide)] = part5[...]


def solution(mesh):
    row_spec = P(('rep', 'dp'), None)
    cache_spec = P(('rep', 'dp'), 'sp', None, None)
    len_spec = P(('rep', 'dp'))

    def local_step(hidden, w_query, w_key, w_value, w_out, k_cache, v_cache, write_pos, valid_len):
        rows, span, kv_heads, dim = k_cache.shape
        model = hidden.shape[1]
        heads = w_query.shape[1] // dim
        cache = (rows, span, dim)
        hbm = lambda a: pltpu.with_memory_space_constraint(a, pltpu.HBM)
        acc, ml, k_new, v_new = pl.pallas_call(
            attend,
            out_shape=[jax.ShapeDtypeStruct((heads, rows, dim), F32),
                       jax.ShapeDtypeStruct((heads, 2 * rows), F32),
                       pltpu.VMEM(cache, BF16), pltpu.VMEM(cache, BF16)],
            in_specs=[ANY] * 8,
            out_specs=[VMEM, VMEM, VMEM, VMEM],
            scratch_shapes=[pltpu.VMEM((rows, model), BF16), pltpu.VMEM(w_query.shape, BF16),
                            pltpu.VMEM(w_key.shape, BF16), pltpu.VMEM(w_value.shape, BF16),
                            pltpu.VMEM((heads, rows, dim), F32), pltpu.VMEM((rows, dim), F32), pltpu.VMEM((rows, dim), F32),
                            pltpu.SMEM((rows,), jnp.int32), pltpu.SMEM((rows,), jnp.int32),
                            pltpu.SemaphoreType.DMA((3 + heads,)), pltpu.SemaphoreType.DMA((2,)),
                            pltpu.SemaphoreType.DMA((rows // GROUP,)), pltpu.SemaphoreType.DMA((rows // GROUP,))],
            compiler_params=pltpu.CompilerParams(vmem_limit_bytes=16 * 2 ** 20),
            cost_estimate=pl.CostEstimate(flops=10 ** 9, bytes_accessed=46 * 10 ** 6, transcendentals=0),
            name='attend',
        )(*map(hbm, (hidden, w_query, w_key, w_value, k_cache.reshape(cache), v_cache.reshape(cache), write_pos, valid_len)))
        wide = w_out.shape[1] // 2
        pair = (2, rows, dim)
        attn_out = pl.pallas_call(
            finish,
            out_shape=jax.ShapeDtypeStruct((rows, w_out.shape[1]), BF16),
            in_specs=[VMEM, VMEM, ANY],
            out_specs=VMEM,
            scratch_shapes=[pltpu.VMEM(w_out.shape, BF16), pltpu.VMEM((3, heads, 2 * rows), F32),
                            pltpu.VMEM((2,) + pair, F32), pltpu.VMEM(pair, F32), pltpu.VMEM(pair, F32), pltpu.VMEM(pair, F32),
                            pltpu.VMEM((2, rows, wide), F32), pltpu.VMEM((rows, wide), F32), pltpu.VMEM((rows, wide), F32),
                            pltpu.VMEM((rows, wide), F32), pltpu.VMEM((rows, wide), BF16), pltpu.VMEM((rows, wide), BF16),
                            pltpu.SemaphoreType.DMA, pltpu.SemaphoreType.DMA((9,)), pltpu.SemaphoreType.DMA((9,))],
            compiler_params=pltpu.CompilerParams(collective_id=0, has_side_effects=True, vmem_limit_bytes=12 * 2 ** 20),
            cost_estimate=pl.CostEstimate(flops=10 ** 9, bytes_accessed=4 * 10 ** 6, transcendentals=0),
            name='finish',
        )(acc, ml, w_out)
        return attn_out, k_new.reshape(k_cache.shape), v_new.reshape(v_cache.shape)

    return jax.shard_map(local_step, mesh=mesh, in_specs=(row_spec, P(), P(), P(), P('sp', None), cache_spec, cache_spec, len_spec, len_spec), out_specs=(row_spec, cache_spec, cache_spec), check_vma=False)
```

time: 129 us -> 49.5 us (0.38)
  Pallas kernels: 0 us -> 35.7 us
  blocking collectives: 30 us -> 0 us
  waiting for transfers between devices: 29.6 us -> 0 us
  matrix products: 27.2 us -> 0 us
  other arithmetic: 25.7 us -> 0 us
  between operations: 14.2 us -> 0.67 us
  local copies, waits for them, and re-layouts: 1.97 us -> 13 us
    pallas_call x0 -> x2, Pallas kernels: none -> 35.7 us  [the longest x1 20 us: local_step(): pl.pallas_call(finish, out_shape=jax.ShapeDtypeStruct((rows, w_out.shape[...]
    psum x1 -> x0, waiting for transfers between devices: 29.6 us -> none  [local_step(): packed = lax.psum(packed, 'sp')]
    dot_general x6 -> x0, matrix products: 27.2 us -> none  [the longest x1 10.3 us: local_step(): jnp.einsum('bkgd,bskd->bkgs', query, k_next, preferred_element_type=jnp.f...]
    select_n x1 -> x0, other arithmetic: 23.1 us -> none  [local_step(): jnp.where(at_pos, value_new.reshape(num_rows, 1, kv_heads, head_dim), v_c...]
    psum x1 -> x0, blocking collectives: 16.7 us -> none  [local_step(): attn_out = lax.psum(partial_out, 'sp').astype(jnp.bfloat16)]
    pmax x1 -> x0, blocking collectives: 13.3 us -> none  [local_step(): global_max = lax.pmax(local_max, 'sp')]
    unnamed x8 -> x5, local copies, waits for them, and re-layouts: 0.12 us -> 13 us
  transfers between devices with their start and end apart: 1 -> 0, of which waited for: 1 -> 0; matrix products, arithmetic and copies ran while one was open for 0% -> 0% of each run, Pallas kernels for 0% -> 0%
where the time goes in v1:
time: 49.5 us; the launch traced here: 49.4 us
  Pallas kernels  35.7 us (72%)
  local copies, waits for them, and re-layouts  13 us (26%)
  between operations  0.67 us (1%)
    pallas_call x1, Pallas kernels, local_step(): pl.pallas_call(finish, out_shape=jax.ShapeDtypeStruct((rows, w_out.shape[...  20 us
    pallas_call x1, Pallas kernels, local_step(): pl.pallas_call(attend, out_shape=[jax.ShapeDtypeStruct((heads, rows, dim)...  15.7 us
    unnamed x5, local copies, waits for them, and re-layouts  13 us

profile of v1, /device:TPU:0, one launch (start us, length us, event | category | flops | bytes accessed | tf_op | source)
XLA Modules:
  0.0 49.4 jit_solution(15501263635097279148)
XLA Ops:
  0.6 0.0 copy-start
  0.6 15.7 %attend.1 = (f32[8,64,256]{2,1,0:T(8,128)S(1)}, f32[8,128]{1,0:T(8,128)S(1)}, bf16[64,512,256]{2,1,0:T(8,128)(2,1)S(1)}, bf16[64,512,256]{2,1,0:T(8,128)(2,1)S(1)}) custom-call(bf16[64,2048]{1,0:T(8,128)(2,1)} %hid_hbm.1, bf16[2048,2048]{1,0:T(8,128)(2,1)} %wq_hbm.1, bf16[2048,256]{1,0:T(8,128)(2,1)} %wk_hbm.1, bf16[2048,256]{1,0:T(8,128)(2,1)} %wv_hbm.1, ...), custom_call_target="tpu_custom_call" | custom-call | flops 1000000000 | bytes 46000000 | tf_op jit(solution)/shard_map/attend/pallas_call | solution.py:196
  16.4 0.0 copy-done
  16.4 20.0 %finish.1 = bf16[64,2048]{1,0:T(8,128)(2,1)S(1)} custom-call(f32[8,64,256]{2,1,0:T(8,128)S(1)} %get-tuple-element.7.acc, f32[8,128]{1,0:T(8,128)S(1)} %get-tuple-element.8.ml, bf16[512,2048]{1,0:T(8,128)(2,1)S(1)} %copy-done), custom_call_target="tpu_custom_call" | custom-call | flops 1000000000 | bytes 4000000 | tf_op jit(solution)/shard_map/finish/pallas_call | solution.py:215
  36.4 6.2 %copy.15 = bf16[64,512,1,256]{3,1,2,0:T(8,128)(2,1)} copy(bf16[64,512,1,256]{3,1,2,0:T(8,128)(2,1)S(1)} %bitcast.9) | data formatting | bytes 33554432
  42.6 6.2 %copy.16 = bf16[64,512,1,256]{3,1,2,0:T(8,128)(2,1)} copy(bf16[64,512,1,256]{3,1,2,0:T(8,128)(2,1)S(1)} %bitcast.8) | data formatting | bytes 33554432
  48.7 0.7 %copy.17 = bf16[64,2048]{1,0:T(8,128)(2,1)} copy(bf16[64,2048]{1,0:T(8,128)(2,1)S(1)} %finish.1) | data formatting | bytes 524288
Async XLA Ops:
  0.6 15.7 %copy-start = (bf16[512,2048]{1,0:T(8,128)(2,1)S(1)}, bf16[512,2048]{1,0:T(8,128)(2,1)}, u32[]{:S(2)}) copy-start(bf16[512,2048]{1,0:T(8,128)(2,1)} %wo_hbm.1) | copy-start | bytes 6291460

commit v2 on v0

v2 whole, which is shorter than its diff:
```python
import functools

import jax
import jax.numpy as jnp
from jax import lax
from jax.experimental import pallas as pl
from jax.experimental.pallas import tpu as pltpu
from jax.sharding import PartitionSpec as P

F32, BF16 = jnp.float32, jnp.bfloat16
NEG_FLOOR = -1e30
GROUP = 8
AHEAD = 4
CHUNKS = ((0, 32), (32, 48), (48, 64))
PLAN = {3: ((0, 0),), 4: ((1, 0),), 5: ((0, 1),), 6: ((2, 0), (1, 1)), 7: ((0, 2), (3, 0)),
        8: ((1, 2), (2, 1), (4, 0), (2, 2), (3, 1), (3, 2), (5, 0), (4, 1), (4, 2), (5, 1), (5, 2))}
ANY = pl.BlockSpec(memory_space=pl.ANY)
VMEM = pl.BlockSpec(memory_space=pltpu.VMEM)
SMEM = pl.BlockSpec(memory_space=pltpu.SMEM)
MESH = pl.DeviceIdType.MESH


def attend(hid_hbm, wq_hbm, wk_hbm, wv_hbm, wo_hbm, k_hbm, v_hbm, pos_hbm, len_hbm,
           att, k_buf, v_buf, k_row, v_row,
           hid, wq, wk, wv, wo, q_all, pos, length, acc, ml, ml_in, part1, send2, part2, mine, half, part3, send4, part4, done, part5,
           sem_w, sem_s, sem_k, sem_v, send, recv):
    rows, span, dim = k_buf.shape
    heads = q_all.shape[0]
    groups = rows // GROUP
    wide = half.shape[2]
    i = lax.axis_index('sp')
    x, c = i // 2, i % 2
    pair, across, far = 2 * x + 1 - c, 2 * (1 - x) + c, 2 * (1 - x) + 1 - c
    start = i * span
    barrier = pltpu.get_barrier_semaphore()
    for peer in (pair, across, far):
        pl.semaphore_signal(barrier, inc=1, device_id={'sp': peer}, device_id_type=MESH)

    def fetch(g):
        part = pl.ds(g * GROUP, GROUP)
        return (pltpu.make_async_copy(k_hbm.at[part], k_buf.at[part], sem_k.at[g]),
                pltpu.make_async_copy(v_hbm.at[part], v_buf.at[part], sem_v.at[g]))

    def q_part(h):
        cols = pl.ds(h * dim, dim)
        return pltpu.make_async_copy(wq_hbm.at[:, cols], wq.at[:, cols], sem_w.at[4 + h])

    scal = [pltpu.make_async_copy(pos_hbm, pos, sem_s.at[0]), pltpu.make_async_copy(len_hbm, length, sem_s.at[1])]
    first = [pltpu.make_async_copy(hid_hbm, hid, sem_w.at[0]),
             pltpu.make_async_copy(wk_hbm, wk, sem_w.at[1]),
             pltpu.make_async_copy(wv_hbm, wv, sem_w.at[2])]
    last = pltpu.make_async_copy(wo_hbm, wo, sem_w.at[3])
    for copy in scal + first + [q_part(h) for h in range(heads)]:
        copy.start()
    for g in range(AHEAD):
        for copy in fetch(g):
            copy.start()
    for copy in scal:
        copy.wait()
    first[0].wait()
    first[1].wait()
    k_row[...] = jnp.dot(hid[...], wk[...], preferred_element_type=F32).astype(BF16).astype(F32)
    first[2].wait()
    v_row[...] = jnp.dot(hid[...], wv[...], preferred_element_type=F32).astype(BF16).astype(F32)
    for h in range(heads):
        q_part(h).wait()
        q_all[h] = jnp.dot(hid[...], wq[:, h * dim:(h + 1) * dim], preferred_element_type=F32).astype(BF16).astype(F32)

    def group_step(g, k):
        for copy in fetch(g):
            copy.wait()
        if g + AHEAD < groups:
            for copy in fetch(g + AHEAD):
                copy.start()
        if g == 0:
            last.start()
        base = g * GROUP
        here = slice(base, base + GROUP)
        q = jnp.swapaxes(q_all[:, here, :], 0, 1)
        fresh = jnp.sum(q * k_row[here, :][:, None, :], axis=2, keepdims=True) * dim ** -0.5
        col = lax.broadcasted_iota(jnp.int32, (heads, span), 1) + start
        lane = lax.broadcasted_iota(jnp.int32, (heads, 128), 1)
        scores = []
        for j in range(GROUP):
            at, end = pos[base + j], length[base + j]
            s = lax.dot_general(q[j].astype(BF16), k_buf[base + j], (((1,), (1,)), ((), ())), preferred_element_type=F32)
            scores.append(jnp.where(jnp.logical_and(col < end, col != at), s * dim ** -0.5, -jnp.inf))
        probs, extra = [], []
        stats = ml[k]
        for j in range(GROUP):
            at, end = pos[base + j], length[base + j]
            owned = jnp.logical_and(jnp.logical_and(at >= start, at < start + span), at < end)
            s_new = jnp.where(owned, fresh[j], -jnp.inf)
            m = jnp.maximum(jnp.maximum(jnp.max(scores[j], axis=1, keepdims=True), s_new), NEG_FLOOR)
            p, p_new = jnp.exp(scores[j] - m), jnp.exp(s_new - m)
            spot = base + j - CHUNKS[k][0]
            stats = jnp.where(lane == spot, m, stats)
            stats = jnp.where(lane == 64 + spot, jnp.sum(p, axis=1, keepdims=True) + p_new, stats)
            probs.append(p.astype(BF16))
            extra.append(p_new)
        ml[k] = stats
        out = [jnp.dot(probs[j], v_buf[base + j], preferred_element_type=F32) + extra[j] * v_row[base + j:base + j + 1, :]
               for j in range(GROUP)]
        acc[:, here, :] = jnp.swapaxes(jnp.stack(out), 0, 1)

    def to(n, k, src, dst, peer):
        return pltpu.make_async_remote_copy(src_ref=src, dst_ref=dst, send_sem=send.at[n, k], recv_sem=recv.at[n, k],
                                            device_id={'sp': peer}, device_id_type=MESH)

    def heads_of(xx, cc):
        return 4 * xx + 2 * cc

    def col_of(v, h):
        lane = lax.broadcasted_iota(jnp.int32, v.shape, 1)
        return jnp.sum(jnp.where(lane == h, v, 0.0), axis=1, keepdims=True)

    def copy_of(n, k):
        r0, r1 = CHUNKS[k]
        rs = pl.ds(r0, r1 - r0)
        if n < 3:
            return to(n, k, ml.at[k], ml_in.at[n, k], (pair, across, far)[n])
        if n == 3:
            return to(n, k, acc.at[pl.ds(heads_of(1 - x, 1 - c), 2), rs], part1.at[0, :, rs], pair)
        if n == 4:
            return to(n, k, acc.at[pl.ds(heads_of(x, 1 - c), 2), rs], part1.at[1, :, rs], pair)
        if n == 5:
            return to(n, k, send2.at[:, rs], part2.at[:, rs], across)
        if n == 6:
            return to(n, k, half.at[0, rs], part3.at[rs], pair)
        if n == 7:
            return to(n, k, send4.at[rs], part4.at[rs], across)
        return to(n, k, done.at[rs], part5.at[rs], pair)

    def stage(n, k):
        r0, r1 = CHUNKS[k]
        size = r1 - r0
        rs = slice(r0, r1)

        def split(v):
            t = v.T
            return t[:size], t[64:64 + size]

        own_cols = pl.ds(pl.multiple_of(c * wide, wide), wide)
        other_cols = pl.ds(pl.multiple_of((1 - c) * wide, wide), wide)
        if n == 0:
            if k == 0:
                pl.semaphore_wait(barrier, 3)
            for q in range(5):
                copy_of(q, k).start()
        elif n == 1:
            copy_of(0, k).wait()
            m0, m1 = split(ml[k])[0], split(ml_in[0, k])[0]
            mp = jnp.maximum(m0, m1)
            e0, e1 = jnp.exp(m0 - mp), jnp.exp(m1 - mp)
            copy_of(3, k).wait()
            for j in range(2):
                h = heads_of(1 - x, c) + j
                send2[j, rs] = acc[h, rs] * col_of(e0, h) + part1[0, j, rs] * col_of(e1, h)
            copy_of(5, k).start()
            copy_of(4, k).wait()
            for j in range(2):
                h = heads_of(x, c) + j
                mine[j, rs] = acc[h, rs] * col_of(e0, h) + part1[1, j, rs] * col_of(e1, h)
        elif n == 2:
            copy_of(1, k).wait()
            copy_of(2, k).wait()
            m0, l0 = split(ml[k])
            m1, l1 = split(ml_in[0, k])
            m2, l2 = split(ml_in[1, k])
            m3, l3 = split(ml_in[2, k])
            mp, mq = jnp.maximum(m0, m1), jnp.maximum(m2, m3)
            mt = jnp.maximum(mp, mq)
            inv = 1.0 / (l0 * jnp.exp(m0 - mt) + l1 * jnp.exp(m1 - mt) + l2 * jnp.exp(m2 - mt) + l3 * jnp.exp(m3 - mt))
            ep, eq = jnp.exp(mp - mt) * inv, jnp.exp(mq - mt) * inv
            heads_here = [heads_of(x, c) + j for j in range(2)]
            factors = [(col_of(ep, h), col_of(eq, h)) for h in heads_here]
            if k == 0:
                last.wait()
            copy_of(5, k).wait()
            o = jnp.concatenate([(mine[j, rs] * factors[j][0] + part2[j, rs] * factors[j][1]).astype(BF16) for j in range(2)], axis=1)
            half[0, rs] = jnp.dot(o, wo[:, other_cols], preferred_element_type=F32)
            copy_of(6, k).start()
            half[1, rs] = jnp.dot(o, wo[:, own_cols], preferred_element_type=F32)
        elif n == 3:
            copy_of(6, k).wait()
            send4[rs] = half[1, rs] + part3[rs]
            copy_of(7, k).start()
        elif n == 4:
            copy_of(7, k).wait()
            done[rs] = (send4[rs] + part4[rs]).astype(BF16)
            copy_of(8, k).start()
            att[rs, own_cols] = done[rs]
        else:
            copy_of(8, k).wait()
            att[rs, other_cols] = part5[rs]

    for k in range(len(CHUNKS)):
        ml[k] = jnp.zeros(ml.shape[1:], F32)
    for g in range(groups):
        group_step(g, [k for k, (r0, r1) in enumerate(CHUNKS) if r0 <= g * GROUP < r1][0])
        for n, k in PLAN.get(g, ()):
            stage(n, k)
    for n, k in PLAN[groups]:
        stage(n, k)


def store(k_in, v_in, k_row, v_row, att, pos, k_out, v_out, att_out, k_buf, v_buf, sem_k, sem_v, sem_a):
    rows, span, dim = k_in.shape
    groups = rows // GROUP
    start = lax.axis_index('sp') * span
    tail = pltpu.make_async_copy(att, att_out, sem_a)
    tail.start()
    sub = lax.broadcasted_iota(jnp.int32, (16, dim), 0)

    def patch(g):
        for b in range(g * GROUP, (g + 1) * GROUP):
            at = pos[b] - start
            inside = jnp.logical_and(at >= 0, at < span)
            at = jnp.where(inside, at, 0)
            win = pl.ds(pl.multiple_of(at // 16 * 16, 16), 16)
            hit = jnp.logical_and(sub == at % 16, inside)
            for row, buf in ((k_row, k_buf), (v_row, v_buf)):
                buf[b, win, :] = jnp.where(hit, row[b:b + 1, :], buf[b, win, :].astype(F32)).astype(BF16)

    def put(g):
        part = pl.ds(g * GROUP, GROUP)
        return (pltpu.make_async_copy(k_buf.at[part], k_out.at[part], sem_k.at[g]),
                pltpu.make_async_copy(v_buf.at[part], v_out.at[part], sem_v.at[g]))

    patch(0)
    for g in range(groups):
        if g + 1 < groups:
            patch(g + 1)
        for copy in put(g):
            copy.start()
    for g in range(groups):
        for copy in put(g):
            copy.wait()
    tail.wait()


def solution(mesh):
    row_spec = P(('rep', 'dp'), None)
    cache_spec = P(('rep', 'dp'), 'sp', None, None)
    len_spec = P(('rep', 'dp'))

    def local_step(hidden, w_query, w_key, w_value, w_out, k_cache, v_cache, write_pos, valid_len):
        rows, span, kv_heads, dim = k_cache.shape
        model = hidden.shape[1]
        heads = w_query.shape[1] // dim
        cache = (rows, span, dim)
        wide = w_out.shape[1] // 2
        pair = (2, rows, dim)
        chunks = len(CHUNKS)
        dma = pltpu.SemaphoreType.DMA
        hbm = lambda a: pltpu.with_memory_space_constraint(a, pltpu.HBM)
        vm = lambda a: pltpu.with_memory_space_constraint(a, pltpu.VMEM)
        att, k_mid, v_mid, k_row, v_row = pl.pallas_call(
            attend,
            out_shape=[pltpu.VMEM((rows, w_out.shape[1]), BF16), pltpu.VMEM(cache, BF16), pltpu.VMEM(cache, BF16),
                       pltpu.VMEM((rows, dim), F32), pltpu.VMEM((rows, dim), F32)],
            in_specs=[ANY] * 9,
            out_specs=[VMEM] * 5,
            scratch_shapes=[pltpu.VMEM((rows, model), BF16), pltpu.VMEM(w_query.shape, BF16),
                            pltpu.VMEM(w_key.shape, BF16), pltpu.VMEM(w_value.shape, BF16), pltpu.VMEM(w_out.shape, BF16),
                            pltpu.VMEM((heads, rows, dim), F32),
                            pltpu.SMEM((rows,), jnp.int32), pltpu.SMEM((rows,), jnp.int32),
                            pltpu.VMEM((heads, rows, dim), F32), pltpu.VMEM((chunks, heads, 128), F32), pltpu.VMEM((3, chunks, heads, 128), F32),
                            pltpu.VMEM((2,) + pair, F32), pltpu.VMEM(pair, F32), pltpu.VMEM(pair, F32), pltpu.VMEM(pair, F32),
                            pltpu.VMEM((2, rows, wide), F32), pltpu.VMEM((rows, wide), F32), pltpu.VMEM((rows, wide), F32),
                            pltpu.VMEM((rows, wide), F32), pltpu.VMEM((rows, wide), BF16), pltpu.VMEM((rows, wide), BF16),
                            dma((4 + heads,)), dma((2,)), dma((rows // GROUP,)), dma((rows // GROUP,)), dma((9, chunks)), dma((9, chunks))],
            compiler_params=pltpu.CompilerParams(collective_id=0, has_side_effects=True, vmem_limit_bytes=24 * 2 ** 20),
            cost_estimate=pl.CostEstimate(flops=10 ** 9, bytes_accessed=46 * 10 ** 6, transcendentals=0),
            name='attend',
        )(*map(hbm, (hidden, w_query, w_key, w_value, w_out, k_cache.reshape(cache), v_cache.reshape(cache), write_pos, valid_len)))
        k_new, v_new, attn_out, _, _ = pl.pallas_call(
            store,
            out_shape=[pltpu.HBM(cache, BF16), pltpu.HBM(cache, BF16), pltpu.HBM(att.shape, BF16), pltpu.VMEM(cache, BF16), pltpu.VMEM(cache, BF16)],
            in_specs=[VMEM] * 5 + [SMEM],
            out_specs=[ANY, ANY, ANY, VMEM, VMEM],
            input_output_aliases={0: 3, 1: 4},
            scratch_shapes=[dma((rows // GROUP,)), dma((rows // GROUP,)), dma],
            compiler_params=pltpu.CompilerParams(vmem_limit_bytes=24 * 2 ** 20),
            cost_estimate=pl.CostEstimate(flops=10 ** 6, bytes_accessed=34 * 10 ** 6, transcendentals=0),
            name='store',
        )(vm(k_mid), vm(v_mid), vm(k_row), vm(v_row), vm(att), write_pos)
        return attn_out, k_new.reshape(k_cache.shape), v_new.reshape(v_cache.shape)

    return jax.shard_map(local_step, mesh=mesh, in_specs=(row_spec, P(), P(), P(), P('sp', None), cache_spec, cache_spec, len_spec, len_spec), out_specs=(row_spec, cache_spec, cache_spec), check_vma=False)
```

time: 129 us -> 45.8 us (0.36)
  Pallas kernels: 0 us -> 45 us
  blocking collectives: 30 us -> 0 us
  waiting for transfers between devices: 29.6 us -> 0 us
  matrix products: 27.2 us -> 0 us
  other arithmetic: 25.7 us -> 0 us
  between operations: 14.2 us -> 0.64 us
  local copies, waits for them, and re-layouts: 1.97 us -> 0 us
    pallas_call x0 -> x2, Pallas kernels: none -> 45 us  [the longest x1 33.1 us: local_step(): pl.pallas_call(attend, out_shape=[pltpu.VMEM((rows, w_out.shape[1]), BF16...]
    psum x1 -> x0, waiting for transfers between devices: 29.6 us -> none  [local_step(): packed = lax.psum(packed, 'sp')]
    dot_general x6 -> x0, matrix products: 27.2 us -> none  [the longest x1 10.3 us: local_step(): jnp.einsum('bkgd,bskd->bkgs', query, k_next, preferred_element_type=jnp.f...]
    select_n x1 -> x0, other arithmetic: 23.1 us -> none  [local_step(): jnp.where(at_pos, value_new.reshape(num_rows, 1, kv_heads, head_dim), v_c...]
    psum x1 -> x0, blocking collectives: 16.7 us -> none  [local_step(): attn_out = lax.psum(partial_out, 'sp').astype(jnp.bfloat16)]
    pmax x1 -> x0, blocking collectives: 13.3 us -> none  [local_step(): global_max = lax.pmax(local_max, 'sp')]
  transfers between devices with their start and end apart: 1 -> 0, of which waited for: 1 -> 0; matrix products, arithmetic and copies ran while one was open for 0% -> 0% of each run, Pallas kernels for 0% -> 0%
where the time goes in v2:
time: 45.8 us; the launch traced here: 45.7 us
  Pallas kernels  45 us (98%)
  between operations  0.64 us (1%)
    pallas_call x1, Pallas kernels, local_step(): pl.pallas_call(attend, out_shape=[pltpu.VMEM((rows, w_out.shape[1]), BF16...  33.1 us
    pallas_call x1, Pallas kernels, local_step(): pl.pallas_call(store, out_shape=[pltpu.HBM(cache, BF16), pltpu.HBM(cache,...  11.9 us

profile of v2, /device:TPU:0, one launch (start us, length us, event | category | flops | bytes accessed | tf_op | source)
XLA Modules:
  0.0 45.7 jit_solution(5864110587546522650)
XLA Ops:
  0.6 33.1 %attend.1 = (bf16[64,2048]{1,0:T(8,128)(2,1)S(1)}, bf16[64,512,256]{2,1,0:T(8,128)(2,1)S(1)}, bf16[64,512,256]{2,1,0:T(8,128)(2,1)S(1)}, f32[64,256]{1,0:T(8,128)S(1)}, f32[64,256]{1,0:T(8,128)S(1)}) custom-call(bf16[64,2048]{1,0:T(8,128)(2,1)} %hid_hbm.1, bf16[2048,2048]{1,0:T(8,128)(2,1)} %wq_hbm.1, bf16[2048,256]{1,0:T(8,128)(2,1)} %wk_hbm.1, ...), custom_call_target="tpu_custom_call" | custom-call | flops 1000000000 | bytes 46000000 | tf_op jit(solution)/shard_map/attend/pallas_call | solution.py:258
  33.8 11.9 %store.1 = (bf16[64,512,256]{2,1,0:T(8,128)(2,1)}, bf16[64,512,256]{2,1,0:T(8,128)(2,1)}, bf16[64,2048]{1,0:T(8,128)(2,1)}, bf16[64,512,256]{2,1,0:T(8,128)(2,1)S(1)}, bf16[64,512,256]{2,1,0:T(8,128)(2,1)S(1)}) custom-call(bf16[64,512,256]{2,1,0:T(8,128)(2,1)S(1)} %get-tuple-element.11.k_in, ...), custom_call_target="tpu_custom_call", output_to_operand_aliasing={{3}: (0, {}), {4}: (1, {})} | custom-call | flops 1000000 | bytes 34000000 | tf_op jit(solution)/shard_map/store/pallas_call | solution.py:277

commit v3 on v0

v3 whole, which is shorter than its diff:
```python
import functools

import jax
import jax.numpy as jnp
from jax import lax
from jax.experimental import pallas as pl
from jax.experimental.pallas import tpu as pltpu
from jax.sharding import PartitionSpec as P


F32, BF16 = jnp.float32, jnp.bfloat16
NEG_FLOOR = -1e30
GROUP = 8
FEED = (1, 1, 2, 2, 2, 2, 2)
LATE = 4
CHUNKS = ((0, 48), (48, 64))
TAIL = ((2, 0), (3, 0), (2, 1), (3, 1))
SPLIT = 16
EARLY = 2
ANY = pl.BlockSpec(memory_space=pl.ANY)
VMEM = pl.BlockSpec(memory_space=pltpu.VMEM)
SMEM = pl.BlockSpec(memory_space=pltpu.SMEM)
MESH = pl.DeviceIdType.MESH


def attend(hid_hbm, wq_hbm, wk_hbm, wv_hbm, wo_hbm, k_hbm, v_hbm, pos_hbm, len_hbm,
           total, k_buf, v_buf, kv_row,
           hid, wq, wkv, wo, q_all, pos, length, acc, ml, ml_in, parts, half, part3,
           sem_w, sem_s, sem_k, sem_v, send_q, recv_q, send_a, recv_a, send, recv):
    rows, span, dim = k_buf.shape
    heads = q_all.shape[0]
    groups = rows // GROUP
    wide = half.shape[2]
    mine = heads // 2
    i = lax.axis_index('sp')
    x, c = i // 2, i % 2
    peers = pair, across, far = 2 * x + 1 - c, 2 * (1 - x) + c, 2 * (1 - x) + 1 - c
    start = i * span
    barrier = pltpu.get_barrier_semaphore()
    for peer in peers:
        pl.semaphore_signal(barrier, inc=1, device_id={'sp': peer}, device_id_type=MESH)

    def fetch(kind, g):
        part = pl.ds(g * GROUP, GROUP)
        if kind == 'o':
            return pltpu.make_async_copy(wo_hbm, wo, sem_w.at[2])
        if kind == 'k':
            return pltpu.make_async_copy(k_hbm.at[part], k_buf.at[part], sem_k.at[g])
        return pltpu.make_async_copy(v_hbm.at[part], v_buf.at[part], sem_v.at[g])

    def q_part(h):
        cols = pl.ds(pl.multiple_of((c * mine + h) * dim, dim), dim)
        return pltpu.make_async_copy(wq_hbm.at[:, cols], wq.at[h], sem_w.at[3 + h])

    def kv_part(hbm):
        return pltpu.make_async_copy(hbm, wkv, sem_w.at[1])

    def to(src, dst, sems, at, peer):
        return pltpu.make_async_remote_copy(src_ref=src, dst_ref=dst, send_sem=sems[0].at[at], recv_sem=sems[1].at[at],
                                            device_id={'sp': peer}, device_id_type=MESH)

    def heads_of(peer):
        return 2 * peer

    scal = [pltpu.make_async_copy(pos_hbm, pos, sem_s.at[0]), pltpu.make_async_copy(len_hbm, length, sem_s.at[1])]
    hidden = pltpu.make_async_copy(hid_hbm, hid, sem_w.at[0])
    hidden.start()

    @pl.when(c == 0)
    def _():
        kv_part(wk_hbm).start()

    @pl.when(c == 1)
    def _():
        kv_part(wv_hbm).start()

    for h in range(mine):
        q_part(h).start()
    for copy in scal:
        copy.start()
    order = [('k', 0)]
    for g in range(1, groups):
        order += [('k', g), ('v', g - 1)]
    order.append(('v', groups - 1))
    order.insert(2 * LATE, ('o', 0))
    started = []

    def begin(count):
        for item in order[len(started):len(started) + count]:
            started.append(item)
            fetch(*item).start()

    begin(FEED[0])
    for copy in scal:
        copy.wait()
    hidden.wait()
    kv_part(wk_hbm).wait()
    begin(FEED[1])
    kv_row[c] = jnp.dot(hid[...], wkv[...], preferred_element_type=F32).astype(BF16).astype(F32)
    for h in range(mine):
        q_part(h).wait()
        begin(FEED[2 + h])
        q_all[c * mine + h] = jnp.dot(hid[...], wq[h], preferred_element_type=F32).astype(BF16).astype(F32)
    for k in range(len(CHUNKS)):
        ml[k] = jnp.zeros(ml.shape[1:], F32)
    pl.semaphore_wait(barrier, 3)
    q_half = q_all.at[pl.ds(c * mine, mine)]
    swaps = [to(kv_row.at[c], kv_row.at[c], (send_q, recv_q), 0, pair), to(q_half, q_half, (send_q, recv_q), 1, pair)]
    for copy in swaps:
        copy.start()
    for copy in swaps:
        copy.wait()

    def score(g):
        base = g * GROUP
        here = slice(base, base + GROUP)
        k = [n for n, (r0, r1) in enumerate(CHUNKS) if r0 <= base < r1][0]
        q = jnp.swapaxes(q_all[:, here, :], 0, 1)
        fresh = jnp.sum(q * kv_row[0, here, :][:, None, :], axis=2, keepdims=True) * dim ** -0.5
        col = lax.broadcasted_iota(jnp.int32, (heads, span), 1) + start
        lane = lax.broadcasted_iota(jnp.int32, (heads, 128), 1)
        scores = []
        for j in range(GROUP):
            at, end = pos[base + j], length[base + j]
            s = lax.dot_general(q[j].astype(BF16), k_buf[base + j], (((1,), (1,)), ((), ())), preferred_element_type=F32)
            scores.append(jnp.where(jnp.logical_and(col < end, col != at), s * dim ** -0.5, -jnp.inf))
        probs, extra = [], []
        stats = ml[k]
        for j in range(GROUP):
            at, end = pos[base + j], length[base + j]
            owned = jnp.logical_and(jnp.logical_and(at >= start, at < start + span), at < end)
            s_new = jnp.where(owned, fresh[j], -jnp.inf)
            m = jnp.maximum(jnp.maximum(jnp.max(scores[j], axis=1, keepdims=True), s_new), NEG_FLOOR)
            p, p_new = jnp.exp(scores[j] - m), jnp.exp(s_new - m)
            spot = base + j - CHUNKS[k][0]
            stats = jnp.where(lane == spot, m, stats)
            stats = jnp.where(lane == 64 + spot, jnp.sum(p, axis=1, keepdims=True) + p_new, stats)
            probs.append(p.astype(BF16))
            extra.append(p_new)
        ml[k] = stats
        return probs, extra

    def blend(g, probs, extra):
        base = g * GROUP
        out = [jnp.dot(probs[j], v_buf[base + j], preferred_element_type=F32) + extra[j] * kv_row[1, base + j:base + j + 1, :]
               for j in range(GROUP)]
        acc[:, base:base + GROUP, :] = jnp.swapaxes(jnp.stack(out), 0, 1)

    def give_acc(g, n):
        rs = pl.ds(g * GROUP, GROUP)
        return to(acc.at[pl.ds(heads_of(peers[n]), 2), rs], parts.at[n, :, rs], (send_a, recv_a), (n, g), peers[n])

    def give(n, k):
        r0, r1 = CHUNKS[k]
        rs = pl.ds(r0, r1 - r0)
        sems = send, recv
        if n < 3:
            return to(ml.at[k], ml_in.at[n, k], sems, (n, k), peers[n])
        return to(half.at[0, rs], part3.at[rs], sems, (n, k), pair)

    own_cols = pl.ds(pl.multiple_of(c * wide, wide), wide)
    other_cols = pl.ds(pl.multiple_of((1 - c) * wide, wide), wide)

    def col_of(v, h):
        lane = lax.broadcasted_iota(jnp.int32, v.shape, 1)
        return jnp.sum(jnp.where(lane == h, v, 0.0), axis=1, keepdims=True)

    def stage(n, k):
        r0, r1 = CHUNKS[k]
        size = r1 - r0
        rs = slice(r0, r1)
        if n == 2:
            for q in range(3):
                give(q, k).wait()
            stats = []
            for v in (ml[k], ml_in[0, k], ml_in[1, k], ml_in[2, k]):
                t = v.T
                stats.append((t[:size], t[64:64 + size]))
            top = functools.reduce(jnp.maximum, [m for m, _ in stats])
            scale = [jnp.exp(m - top) for m, _ in stats]
            inv = 1.0 / functools.reduce(jnp.add, [l * e for (_, l), e in zip(stats, scale)])
            scale = [e * inv for e in scale]
            cols = [[col_of(e, heads_of(i) + j) for e in scale] for j in range(2)]
            if k == 0:
                fetch('o', 0).wait()
            for q in range(3):
                for g in range(r0 // GROUP, r1 // GROUP):
                    give_acc(g, q).wait()
            o = []
            for j in range(2):
                part = acc[heads_of(i) + j, rs] * cols[j][0]
                for q in range(3):
                    part += parts[q, j, rs] * cols[j][q + 1]
                o.append(part.astype(BF16))
            o = jnp.concatenate(o, axis=1)
            half[0, rs] = jnp.dot(o, wo[:, other_cols], preferred_element_type=F32)
            give(3, k).start()
            half[1, rs] = jnp.dot(o, wo[:, own_cols], preferred_element_type=F32)
        else:
            give(3, k).wait()
            total[rs] = half[1, rs] + part3[rs]

    fetch('k', 0).wait()
    held = score(0)
    for g in range(groups):
        if g + 1 < groups:
            fetch('k', g + 1).wait()
        fetch('v', g).wait()
        begin(FEED[-1])
        following = score(g + 1) if g + 1 < groups else None
        blend(g, *held)
        held = following
        for n in range(3):
            give_acc(g, n).start()
        for k, (r0, r1) in enumerate(CHUNKS):
            if r1 == (g + 1) * GROUP:
                for n in range(3):
                    give(n, k).start()
    for n, k in TAIL:
        stage(n, k)


def store(jobs, kv_row, pos_hbm, bufs, outs, pos, sem_p, sem_g, sem_w):
    span, dim = bufs[0].shape[1:]
    start = lax.axis_index('sp') * span
    sub = lax.broadcasted_iota(jnp.int32, (16, dim), 0)
    cuts = [(n, r) for n, r0, r1 in jobs for r in range(r0, r1, GROUP)]

    def place(b):
        at = pos[b] - start
        inside = jnp.logical_and(at >= 0, at < span)
        at = jnp.where(inside, at, 0)
        return at, inside, pl.ds(pl.multiple_of(at // 16 * 16, 16), 16)

    def patch(n, r):
        for b in range(r, r + GROUP):
            at, inside, win = place(b)
            hit = jnp.logical_and(sub == at % 16, inside)
            bufs[n][b, win, :] = jnp.where(hit, kv_row[n, b:b + 1, :], bufs[n][b, win, :].astype(F32)).astype(BF16)

    def put(n, r):
        part = pl.ds(r, GROUP)
        return pltpu.make_async_copy(bufs[n].at[part], outs[n].at[part], sem_g.at[n, r // GROUP])

    def windows(n, r, act):
        for b in range(r, r + GROUP):
            _, inside, win = place(b)

            @pl.when(inside)
            def _():
                act(pltpu.make_async_copy(bufs[n].at[b, win], outs[n].at[b, win], sem_w.at[b - cuts[0][1]]))

    ask = pltpu.make_async_copy(pos_hbm, pos, sem_p)
    ask.start()
    early, later = cuts[:EARLY], cuts[EARLY:]
    for cut in early:
        put(*cut).start()
    ask.wait()
    for cut in later:
        patch(*cut)
        put(*cut).start()
    for cut in early:
        put(*cut).wait()
        patch(*cut)
        windows(*cut, lambda copy: copy.start())
    for cut in later:
        put(*cut).wait()
    for cut in early:
        windows(*cut, lambda copy: copy.wait())


def store_first(k_in, v_in, kv_row, pos_hbm, k_out, v_out, k_buf, v_buf, *rest, jobs):
    store(jobs, kv_row, pos_hbm, (k_buf, v_buf), (k_out, v_out), *rest)


def store_second(v_in, kv_row, pos_hbm, v_old, v_out, v_buf, *rest, jobs):
    store(jobs, kv_row, pos_hbm, (v_buf, v_buf), (v_out, v_out), *rest)


def final(own, other, pair_own, pair_other, out):
    wide = own.shape[1]
    c = lax.axis_index('sp') % 2
    out[:, pl.ds(pl.multiple_of(c * wide, wide), wide)] = (own[...] + other[...]).astype(BF16)
    out[:, pl.ds(pl.multiple_of((1 - c) * wide, wide), wide)] = (pair_own[...] + pair_other[...]).astype(BF16)


def solution(mesh):
    row_spec = P(('rep', 'dp'), None)
    cache_spec = P(('rep', 'dp'), 'sp', None, None)
    len_spec = P(('rep', 'dp'))

    def one_step(hidden, w_query, w_key, w_value, w_out, k_cache, v_cache, write_pos, valid_len):
        rows, span, _, dim = k_cache.shape
        model = hidden.shape[1]
        heads = w_query.shape[1] // dim
        cache = (rows, span, dim)
        wide = w_out.shape[1] // 2
        pair = (2, rows, dim)
        chunks = len(CHUNKS)
        dma = pltpu.SemaphoreType.DMA
        hbm = lambda a: pltpu.with_memory_space_constraint(a, pltpu.HBM)
        vm = lambda a: pltpu.with_memory_space_constraint(a, pltpu.VMEM)
        total, k_mid, v_mid, kv_row = pl.pallas_call(
            attend,
            out_shape=[pltpu.VMEM((rows, wide), F32), pltpu.VMEM(cache, BF16), pltpu.VMEM(cache, BF16),
                       pltpu.VMEM((2, rows, dim), F32)],
            in_specs=[ANY] * 9,
            out_specs=[VMEM] * 4,
            scratch_shapes=[pltpu.VMEM((rows, model), BF16), pltpu.VMEM((heads // 2, model, dim), BF16),
                            pltpu.VMEM(w_key.shape, BF16), pltpu.VMEM(w_out.shape, BF16),
                            pltpu.VMEM((heads, rows, dim), F32),
                            pltpu.SMEM((rows,), jnp.int32), pltpu.SMEM((rows,), jnp.int32),
                            pltpu.VMEM((heads, rows, dim), F32), pltpu.VMEM((chunks, heads, 128), F32), pltpu.VMEM((3, chunks, heads, 128), F32),
                            pltpu.VMEM((3,) + pair, F32),
                            pltpu.VMEM((2, rows, wide), F32), pltpu.VMEM((rows, wide), F32),
                            dma((3 + heads // 2,)), dma((2,)), dma((rows // GROUP,)), dma((rows // GROUP,)), dma((2,)), dma((2,)),
                            dma((3, rows // GROUP)), dma((3, rows // GROUP)), dma((4, chunks)), dma((4, chunks))],
            compiler_params=pltpu.CompilerParams(collective_id=0, has_side_effects=True, vmem_limit_bytes=12 * 2 ** 20),
            cost_estimate=pl.CostEstimate(flops=10 ** 9, bytes_accessed=46 * 10 ** 6, transcendentals=0),
            name='attend',
        )(*map(hbm, (hidden, w_query, w_key, w_value, w_out, k_cache.reshape(cache), v_cache.reshape(cache), write_pos, valid_len)))
        across = [(d, (d + 2) % 4) for d in range(4)]
        pairs = [(d, d ^ 1) for d in range(4)]
        other = lax.ppermute(total, 'sp', across)
        pair_own = lax.ppermute(total, 'sp', pairs)
        pair_other = lax.ppermute(other, 'sp', pairs)
        common = dict(
            scratch_shapes=[pltpu.SMEM((rows,), jnp.int32), dma, dma((2, rows // GROUP)), dma((EARLY * GROUP,))],
            compiler_params=pltpu.CompilerParams(vmem_limit_bytes=12 * 2 ** 20))
        full, held = pltpu.HBM(cache, BF16), pltpu.VMEM(cache, BF16)
        k_new, v_part, _, v_mid = pl.pallas_call(
            functools.partial(store_first, jobs=((0, 0, rows), (1, 0, SPLIT))),
            out_shape=[full, full, held, held], in_specs=[VMEM] * 3 + [ANY], out_specs=[ANY, ANY, VMEM, VMEM],
            input_output_aliases={0: 2, 1: 3}, name='store_first',
            cost_estimate=pl.CostEstimate(flops=10 ** 9, bytes_accessed=21 * 10 ** 6, transcendentals=0), **common,
        )(vm(k_mid), vm(v_mid), vm(kv_row), hbm(write_pos))
        v_new, _ = pl.pallas_call(
            functools.partial(store_second, jobs=((1, SPLIT, rows),)),
            out_shape=[full, held], in_specs=[VMEM, VMEM, ANY, ANY], out_specs=[ANY, VMEM],
            input_output_aliases={0: 1, 3: 0}, name='store_second',
            cost_estimate=pl.CostEstimate(flops=6 * 10 ** 8, bytes_accessed=13 * 10 ** 6, transcendentals=0), **common,
        )(vm(v_mid), vm(kv_row), hbm(write_pos), v_part)
        attn_out = pl.pallas_call(
            final,
            out_shape=jax.ShapeDtypeStruct((rows, w_out.shape[1]), BF16),
            in_specs=[VMEM] * 4,
            out_specs=VMEM,
            compiler_params=pltpu.CompilerParams(vmem_limit_bytes=4 * 2 ** 20),
            cost_estimate=pl.CostEstimate(flops=10 ** 6, bytes_accessed=2 ** 20, transcendentals=0),
            name='final',
        )(total, other, pair_own, pair_other)
        return attn_out, k_new.reshape(k_cache.shape), v_new.reshape(v_cache.shape)

    return jax.shard_map(one_step, mesh=mesh, in_specs=(row_spec, P(), P(), P(), P('sp', None), cache_spec, cache_spec, len_spec, len_spec), out_specs=(row_spec, cache_spec, cache_spec), check_vma=False)
```

time: 129 us -> 44 us (0.34)
  Pallas kernels: 0 us -> 34.8 us
  blocking collectives: 30 us -> 0 us
  matrix products: 27.2 us -> 0 us
  other arithmetic: 25.7 us -> 0 us
  waiting for transfers between devices: 29.6 us -> 8.18 us
  between operations: 14.2 us -> 0.68 us
  local copies, waits for them, and re-layouts: 1.97 us -> 0 us
    pallas_call x0 -> x4, Pallas kernels: none -> 34.8 us  [the longest x1 21.7 us: one_step(): pl.pallas_call(attend, out_shape=[pltpu.VMEM((rows, wide), F32), pltpu.VM...]
    psum x1 -> x0, waiting for transfers between devices: 29.6 us -> none  [local_step(): packed = lax.psum(packed, 'sp')]
    dot_general x6 -> x0, matrix products: 27.2 us -> none  [the longest x1 10.3 us: local_step(): jnp.einsum('bkgd,bskd->bkgs', query, k_next, preferred_element_type=jnp.f...]
    select_n x1 -> x0, other arithmetic: 23.1 us -> none  [local_step(): jnp.where(at_pos, value_new.reshape(num_rows, 1, kv_heads, head_dim), v_c...]
    psum x1 -> x0, blocking collectives: 16.7 us -> none  [local_step(): attn_out = lax.psum(partial_out, 'sp').astype(jnp.bfloat16)]
    pmax x1 -> x0, blocking collectives: 13.3 us -> none  [local_step(): global_max = lax.pmax(local_max, 'sp')]
    ppermute x0 -> x3, waiting for transfers between devices: none -> 8.18 us  [the longest x1 8.18 us: one_step(): other = lax.ppermute(total, 'sp', across)]
  transfers between devices with their start and end apart: 1 -> 3, of which waited for: 1 -> 1; matrix products, arithmetic and copies ran while one was open for 0% -> 0% of each run, Pallas kernels for 0% -> 28%
where the time goes in v3:
time: 44 us; the launch traced here: 43.9 us
  Pallas kernels  34.8 us (79%)
  waiting for transfers between devices  8.18 us (19%)
  between operations  0.68 us (2%)
    pallas_call x1, Pallas kernels, one_step(): pl.pallas_call(attend, out_shape=[pltpu.VMEM((rows, wide), F32), pltpu.VM...  21.7 us
    ppermute x1, waiting for transfers between devices, one_step(): other = lax.ppermute(total, 'sp', across)  8.18 us
    pallas_call x1, Pallas kernels, one_step(): pl.pallas_call(functools.partial(store_first, jobs=((0, 0, rows), (1, 0,...  7.41 us
    pallas_call x1, Pallas kernels, one_step(): pl.pallas_call(functools.partial(store_second, jobs=((1, SPLIT, rows),)),...  4.89 us
  transfers between devices with their start and end apart: 3, of which 1 were waited for; matrix products, arithmetic and copies ran while one was open for 0% of the time, Pallas kernels for 28%

profile of v3, /device:TPU:0, one launch (start us, length us, event | category | flops | bytes accessed | tf_op | source)
XLA Modules:
  0.0 43.9 jit_solution(12968818249816898058)
XLA Ops:
  0.6 21.7 %attend.1 = (f32[64,1024]{1,0:T(8,128)S(1)}, bf16[64,512,256]{2,1,0:T(8,128)(2,1)S(1)}, bf16[64,512,256]{2,1,0:T(8,128)(2,1)S(1)}, f32[2,64,256]{2,1,0:T(8,128)S(1)}) custom-call(bf16[64,2048]{1,0:T(8,128)(2,1)} %hid_hbm.1, bf16[2048,2048]{1,0:T(8,128)(2,1)} %wq_hbm.1, bf16[2048,256]{1,0:T(8,128)(2,1)} %wk_hbm.1, bf16[2048,256]{1,0:T(8,128)(2,1)} %wv_hbm.1, ...), custom_call_target="tpu_custom_call" | custom-call | flops 1000000000 | bytes 46000000 | tf_op jit(solution)/shard_map/attend/pallas_call | solution.py:303
  22.4 0.0 collective-permute-start
  22.4 0.2 collective-permute-start.1
  22.6 8.2 %collective-permute-done.other = f32[64,1024]{1,0:T(8,128)S(1)} collective-permute-done((f32[64,1024]{1,0:T(8,128)S(1)}, f32[64,1024]{1,0:T(8,128)S(1)}, u32[]{:S(2)}, u32[]{:S(2)}) %collective-permute-start) | collective-permute-done | bytes 262176 | tf_op jit(solution)/shard_map/ppermute | solution.py:324
  30.8 0.0 collective-permute-start.2
  30.8 7.4 %store_first.1 = (bf16[64,512,256]{2,1,0:T(8,128)(2,1)}, bf16[64,512,256]{2,1,0:T(8,128)(2,1)}, bf16[64,512,256]{2,1,0:T(8,128)(2,1)S(1)}, bf16[64,512,256]{2,1,0:T(8,128)(2,1)S(1)}) custom-call(bf16[64,512,256]{2,1,0:T(8,128)(2,1)S(1)} %get-tuple-element.12.k_in, ...), custom_call_target="tpu_custom_call", output_to_operand_aliasing={{2}: (0, {}), {3}: (1, {})} | custom-call | flops 1000000000 | bytes 21000000 | tf_op jit(solution)/shard_map/store_first/pallas_call | solution.py:331
  38.2 4.9 %store_second.1 = (bf16[64,512,256]{2,1,0:T(8,128)(2,1)}, bf16[64,512,256]{2,1,0:T(8,128)(2,1)S(1)}) custom-call(bf16[64,512,256]{2,1,0:T(8,128)(2,1)S(1)} %get-tuple-element.16.v_in, f32[2,64,256]{2,1,0:T(8,128)S(1)} %get-tuple-element.14.kv_row, s32[64]{0:T(128)} %pos_hbm.5, ...), custom_call_target="tpu_custom_call", output_to_operand_aliasing={{1}: (0, {}), {0}: (3, {})} | custom-call | flops 600000000 | bytes 13000000 | tf_op jit(solution)/shard_map/store_second/pallas_call | solution.py:337
  43.1 0.0 collective-permute-done.1.pair_own
  43.1 0.0 collective-permute-done.2.pair_other
  43.1 0.8 %final.1 = bf16[64,2048]{1,0:T(8,128)(2,1)} custom-call(f32[64,1024]{1,0:T(8,128)S(1)} %get-tuple-element.11.own, f32[64,1024]{1,0:T(8,128)S(1)} %collective-permute-done.other, f32[64,1024]{1,0:T(8,128)S(1)} %collective-permute-done.1.pair_own, f32[64,1024]{1,0:T(8,128)S(1)} %collective-permute-done.2.pair_other), custom_call_target="tpu_custom_call" | custom-call | flops 1000000 | bytes 1048576 | tf_op jit(solution)/shard_map/final/pallas_call | solution.py:343
Async XLA Ops:
  22.4 8.4 %collective-permute-start = (f32[64,1024]{1,0:T(8,128)S(1)}, f32[64,1024]{1,0:T(8,128)S(1)}, u32[]{:S(2)}, u32[]{:S(2)}) collective-permute-start(f32[64,1024]{1,0:T(8,128)S(1)} %get-tuple-element.11.own), channel_id=1, source_target_pairs={{0,2},{1,3},{2,0},{3,1},{4,6},{5,7},{6,4},{7,5}} | collective-permute-start | bytes 786440 | tf_op jit(solution)/shard_map/ppermute | solution.py:324
  22.4 20.7 %collective-permute-start.1 = (f32[64,1024]{1,0:T(8,128)S(1)}, f32[64,1024]{1,0:T(8,128)S(1)}, u32[]{:S(2)}, u32[]{:S(2)}) collective-permute-start(f32[64,1024]{1,0:T(8,128)S(1)} %get-tuple-element.11.own), channel_id=1, source_target_pairs={{0,1},{1,0},{2,3},{3,2},{4,5},{5,4},{6,7},{7,6}} | collective-permute-start | bytes 786440 | tf_op jit(solution)/shard_map/ppermute | solution.py:325
  30.8 12.3 %collective-permute-start.2 = (f32[64,1024]{1,0:T(8,128)S(1)}, f32[64,1024]{1,0:T(8,128)S(1)}, u32[]{:S(2)}, u32[]{:S(2)}) collective-permute-start(f32[64,1024]{1,0:T(8,128)S(1)} %collective-permute-done.other), channel_id=1, source_target_pairs={{0,1},{1,0},{2,3},{3,2},{4,5},{5,4},{6,7},{7,6}} | collective-permute-start | bytes 786440 | tf_op jit(solution)/shard_map/ppermute | solution.py:326

commit v4 on v3

--- a/solution.py
+++ b/solution.py
@@ -12,11 +12,10 @@
 NEG_FLOOR = -1e30
 GROUP = 8
 FEED = (1, 1, 2, 2, 2, 2, 2)
-LATE = 4
+LATE = 6
 CHUNKS = ((0, 48), (48, 64))
-TAIL = ((2, 0), (3, 0), (2, 1), (3, 1))
-SPLIT = 16
-EARLY = 2
+SPLIT = 48
+EARLY = 1
 ANY = pl.BlockSpec(memory_space=pl.ANY)
 VMEM = pl.BlockSpec(memory_space=pltpu.VMEM)
 SMEM = pl.BlockSpec(memory_space=pltpu.SMEM)
@@ -30,7 +29,7 @@
     rows, span, dim = k_buf.shape
     heads = q_all.shape[0]
     groups = rows // GROUP
-    wide = half.shape[2]
+    wide = half.shape[1]
     mine = heads // 2
     i = lax.axis_index('sp')
     x, c = i // 2, i % 2
@@ -46,7 +45,9 @@
             return pltpu.make_async_copy(wo_hbm, wo, sem_w.at[2])
         if kind == 'k':
             return pltpu.make_async_copy(k_hbm.at[part], k_buf.at[part], sem_k.at[g])
-        return pltpu.make_async_copy(v_hbm.at[part], v_buf.at[part], sem_v.at[g])
+        if g == groups - 1:
+            part = pl.ds(g * GROUP + (kind == 'w') * GROUP // 2, GROUP // 2)
+        return pltpu.make_async_copy(v_hbm.at[part], v_buf.at[part], sem_v.at[g + (kind == 'w')])
 
     def q_part(h):
         cols = pl.ds(pl.multiple_of((c * mine + h) * dim, dim), dim)
@@ -81,7 +82,7 @@
     order = [('k', 0)]
     for g in range(1, groups):
         order += [('k', g), ('v', g - 1)]
-    order.append(('v', groups - 1))
+    order += [('v', groups - 1), ('w', groups - 1)]
     order.insert(2 * LATE, ('o', 0))
     started = []
 
@@ -142,8 +143,11 @@
 
     def blend(g, probs, extra):
         base = g * GROUP
-        out = [jnp.dot(probs[j], v_buf[base + j], preferred_element_type=F32) + extra[j] * kv_row[1, base + j:base + j + 1, :]
-               for j in range(GROUP)]
+        out = []
+        for j in range(GROUP):
+            if g == groups - 1 and j == GROUP // 2:
+                fetch('w', g).wait()
+            out.append(jnp.dot(probs[j], v_buf[base + j], preferred_element_type=F32) + extra[j] * kv_row[1, base + j:base + j + 1, :])
         acc[:, base:base + GROUP, :] = jnp.swapaxes(jnp.stack(out), 0, 1)
 
     def give_acc(g, n):
@@ -156,7 +160,7 @@
         sems = send, recv
         if n < 3:
             return to(ml.at[k], ml_in.at[n, k], sems, (n, k), peers[n])
-        return to(half.at[0, rs], part3.at[rs], sems, (n, k), pair)
+        return to(half, part3, sems, (n, k), pair)
 
     own_cols = pl.ds(pl.multiple_of(c * wide, wide), wide)
     other_cols = pl.ds(pl.multiple_of((1 - c) * wide, wide), wide)
@@ -165,40 +169,34 @@
         lane = lax.broadcasted_iota(jnp.int32, v.shape, 1)
         return jnp.sum(jnp.where(lane == h, v, 0.0), axis=1, keepdims=True)
 
-    def stage(n, k):
+    def combine(k):
         r0, r1 = CHUNKS[k]
         size = r1 - r0
         rs = slice(r0, r1)
-        if n == 2:
+        for q in range(3):
+            give(q, k).wait()
+        stats = []
+        for v in (ml[k], ml_in[0, k], ml_in[1, k], ml_in[2, k]):
+            t = v.T
+            stats.append((t[:size], t[64:64 + size]))
+        top = functools.reduce(jnp.maximum, [m for m, _ in stats])
+        scale = [jnp.exp(m - top) for m, _ in stats]
+        inv = 1.0 / functools.reduce(jnp.add, [l * e for (_, l), e in zip(stats, scale)])
+        scale = [e * inv for e in scale]
+        cols = [[col_of(e, heads_of(i) + j) for e in scale] for j in range(2)]
+        if k == 0:
+            fetch('o', 0).wait()
+        for q in range(3):
+            for g in range(r0 // GROUP, r1 // GROUP):
+                give_acc(g, q).wait()
+        o = []
+        for j in range(2):
+            part = acc[heads_of(i) + j, rs] * cols[j][0]
             for q in range(3):
-                give(q, k).wait()
-            stats = []
-            for v in (ml[k], ml_in[0, k], ml_in[1, k], ml_in[2, k]):
-                t = v.T
-                stats.append((t[:size], t[64:64 + size]))
-            top = functools.reduce(jnp.maximum, [m for m, _ in stats])
-            scale = [jnp.exp(m - top) for m, _ in stats]
-            inv = 1.0 / functools.reduce(jnp.add, [l * e for (_, l), e in zip(stats, scale)])
-            scale = [e * inv for e in scale]
-            cols = [[col_of(e, heads_of(i) + j) for e in scale] for j in range(2)]
-            if k == 0:
-                fetch('o', 0).wait()
-            for q in range(3):
-                for g in range(r0 // GROUP, r1 // GROUP):
-                    give_acc(g, q).wait()
-            o = []
-            for j in range(2):
-                part = acc[heads_of(i) + j, rs] * cols[j][0]
-                for q in range(3):
-                    part += parts[q, j, rs] * cols[j][q + 1]
-                o.append(part.astype(BF16))
-            o = jnp.concatenate(o, axis=1)
-            half[0, rs] = jnp.dot(o, wo[:, other_cols], preferred_element_type=F32)
-            give(3, k).start()
-            half[1, rs] = jnp.dot(o, wo[:, own_cols], preferred_element_type=F32)
-        else:
-            give(3, k).wait()
-            total[rs] = half[1, rs] + part3[rs]
+                part += parts[q, j, rs] * cols[j][q + 1]
+            o.append(part.astype(BF16))
+        o = jnp.concatenate(o, axis=1)
+        return o
 
     fetch('k', 0).wait()
     held = score(0)
@@ -210,14 +208,22 @@
         following = score(g + 1) if g + 1 < groups else None
         blend(g, *held)
         held = following
-        for n in range(3):
-            give_acc(g, n).start()
         for k, (r0, r1) in enumerate(CHUNKS):
             if r1 == (g + 1) * GROUP:
-                for n in range(3):
+                for n in (1, 2, 0):
                     give(n, k).start()
-    for n, k in TAIL:
-        stage(n, k)
+        for n in (1, 2, 0):
+            give_acc(g, n).start()
+    o = combine(0)
+    early = CHUNKS[0][1]
+    half[...] = jnp.dot(o, wo[:, other_cols], preferred_element_type=F32)
+    give(3, 0).start()
+    total[:early] = jnp.dot(o, wo[:, own_cols], preferred_element_type=F32)
+    give(3, 0).wait()
+    total[:early] += part3[...]
+    o = combine(1)
+    total[early:rows] = jnp.dot(o, wo[:, own_cols], preferred_element_type=F32)
+    total[rows:] = jnp.dot(o, wo[:, other_cols], preferred_element_type=F32)
 
 
 def store(jobs, kv_row, pos_hbm, bufs, outs, pos, sem_p, sem_g, sem_w):
@@ -278,10 +284,16 @@
 
 
 def final(own, other, pair_own, pair_other, out):
-    wide = own.shape[1]
+    rows, wide = out.shape[0], own.shape[1]
+    early = CHUNKS[0][1]
     c = lax.axis_index('sp') % 2
-    out[:, pl.ds(pl.multiple_of(c * wide, wide), wide)] = (own[...] + other[...]).astype(BF16)
-    out[:, pl.ds(pl.multiple_of((1 - c) * wide, wide), wide)] = (pair_own[...] + pair_other[...]).astype(BF16)
+    own_cols = pl.ds(pl.multiple_of(c * wide, wide), wide)
+    other_cols = pl.ds(pl.multiple_of((1 - c) * wide, wide), wide)
+    a, b = slice(early, rows), slice(rows, 2 * rows - early)
+    out[:early, own_cols] = (own[:early] + other[:early]).astype(BF16)
+    out[:early, other_cols] = (pair_own[:early] + pair_other[:early]).astype(BF16)
+    out[early:, own_cols] = ((own[a] + pair_own[b]) + (other[a] + pair_other[b])).astype(BF16)
+    out[early:, other_cols] = ((own[b] + pair_own[a]) + (other[b] + pair_other[a])).astype(BF16)
 
 
 def solution(mesh):
@@ -302,7 +314,7 @@
         vm = lambda a: pltpu.with_memory_space_constraint(a, pltpu.VMEM)
         total, k_mid, v_mid, kv_row = pl.pallas_call(
             attend,
-            out_shape=[pltpu.VMEM((rows, wide), F32), pltpu.VMEM(cache, BF16), pltpu.VMEM(cache, BF16),
+            out_shape=[pltpu.VMEM((2 * rows - CHUNKS[0][1], wide), F32), pltpu.VMEM(cache, BF16), pltpu.VMEM(cache, BF16),
                        pltpu.VMEM((2, rows, dim), F32)],
             in_specs=[ANY] * 9,
             out_specs=[VMEM] * 4,
@@ -312,8 +324,8 @@
                             pltpu.SMEM((rows,), jnp.int32), pltpu.SMEM((rows,), jnp.int32),
                             pltpu.VMEM((heads, rows, dim), F32), pltpu.VMEM((chunks, heads, 128), F32), pltpu.VMEM((3, chunks, heads, 128), F32),
                             pltpu.VMEM((3,) + pair, F32),
-                            pltpu.VMEM((2, rows, wide), F32), pltpu.VMEM((rows, wide), F32),
-                            dma((3 + heads // 2,)), dma((2,)), dma((rows // GROUP,)), dma((rows // GROUP,)), dma((2,)), dma((2,)),
+                            pltpu.VMEM((CHUNKS[0][1], wide), F32), pltpu.VMEM((CHUNKS[0][1], wide), F32),
+                            dma((3 + heads // 2,)), dma((2,)), dma((rows // GROUP,)), dma((rows // GROUP + 1,)), dma((2,)), dma((2,)),
                             dma((3, rows // GROUP)), dma((3, rows // GROUP)), dma((4, chunks)), dma((4, chunks))],
             compiler_params=pltpu.CompilerParams(collective_id=0, has_side_effects=True, vmem_limit_bytes=12 * 2 ** 20),
             cost_estimate=pl.CostEstimate(flops=10 ** 9, bytes_accessed=46 * 10 ** 6, transcendentals=0),

time: 44 us -> 43.8 us (level)
  Pallas kernels: 34.8 us -> 33.3 us
  waiting for transfers between devices: 8.18 us -> 9.53 us
    pallas_call x1, Pallas kernels: 4.89 us -> 2.28 us  [one_step(): pl.pallas_call(functools.partial(store_second, jobs=((1, SPLIT, rows),)),...]
    pallas_call x1, Pallas kernels: 7.41 us -> 9.9 us  [one_step(): pl.pallas_call(functools.partial(store_first, jobs=((0, 0, rows), (1, 0,...]
    pallas_call x1, Pallas kernels: 21.7 us -> 20.3 us  [one_step(): pl.pallas_call(attend, out_shape=[pltpu.VMEM((2 * rows - CHUNKS[0][1], wi...]
    ppermute x1, waiting for transfers between devices: 8.18 us -> 9.52 us  [one_step(): other = lax.ppermute(total, 'sp', across)]
where the time goes in v4:
time: 43.8 us; the launch traced here: 43.7 us
  Pallas kernels  33.3 us (76%)
  waiting for transfers between devices  9.53 us (22%)
  between operations  0.67 us (2%)
    pallas_call x1, Pallas kernels, one_step(): pl.pallas_call(attend, out_shape=[pltpu.VMEM((2 * rows - CHUNKS[0][1], wi...  20.3 us
    pallas_call x1, Pallas kernels, one_step(): pl.pallas_call(functools.partial(store_first, jobs=((0, 0, rows), (1, 0,...  9.9 us
    ppermute x1, waiting for transfers between devices, one_step(): other = lax.ppermute(total, 'sp', across)  9.52 us
    pallas_call x1, Pallas kernels, one_step(): pl.pallas_call(functools.partial(store_second, jobs=((1, SPLIT, rows),)),...  2.28 us
  transfers between devices with their start and end apart: 3, of which 1 were waited for; matrix products, arithmetic and copies ran while one was open for 0% of the time, Pallas kernels for 28%

profile of v4, /device:TPU:0, one launch (start us, length us, event | category | flops | bytes accessed | tf_op | source)
XLA Modules:
  0.0 43.7 jit_solution(14841487922994138463)
XLA Ops:
  0.6 20.3 %attend.1 = (f32[80,1024]{1,0:T(8,128)S(1)}, bf16[64,512,256]{2,1,0:T(8,128)(2,1)S(1)}, bf16[64,512,256]{2,1,0:T(8,128)(2,1)S(1)}, f32[2,64,256]{2,1,0:T(8,128)S(1)}) custom-call(bf16[64,2048]{1,0:T(8,128)(2,1)} %hid_hbm.1, bf16[2048,2048]{1,0:T(8,128)(2,1)} %wq_hbm.1, bf16[2048,256]{1,0:T(8,128)(2,1)} %wk_hbm.1, bf16[2048,256]{1,0:T(8,128)(2,1)} %wv_hbm.1, ...), custom_call_target="tpu_custom_call" | custom-call | flops 1000000000 | bytes 46000000 | tf_op jit(solution)/shard_map/attend/pallas_call | solution.py:315
  21.0 0.2 collective-permute-start
  21.1 0.1 collective-permute-start.1
  21.2 9.5 %collective-permute-done.other = f32[80,1024]{1,0:T(8,128)S(1)} collective-permute-done((f32[80,1024]{1,0:T(8,128)S(1)}, f32[80,1024]{1,0:T(8,128)S(1)}, u32[]{:S(2)}, u32[]{:S(2)}) %collective-permute-start) | collective-permute-done | bytes 327712 | tf_op jit(solution)/shard_map/ppermute | solution.py:336
  30.8 0.0 collective-permute-start.2
  30.8 9.9 %store_first.1 = (bf16[64,512,256]{2,1,0:T(8,128)(2,1)}, bf16[64,512,256]{2,1,0:T(8,128)(2,1)}, bf16[64,512,256]{2,1,0:T(8,128)(2,1)S(1)}, bf16[64,512,256]{2,1,0:T(8,128)(2,1)S(1)}) custom-call(bf16[64,512,256]{2,1,0:T(8,128)(2,1)S(1)} %get-tuple-element.12.k_in, ...), custom_call_target="tpu_custom_call", output_to_operand_aliasing={{2}: (0, {}), {3}: (1, {})} | custom-call | flops 1000000000 | bytes 21000000 | tf_op jit(solution)/shard_map/store_first/pallas_call | solution.py:343
  40.7 2.3 %store_second.1 = (bf16[64,512,256]{2,1,0:T(8,128)(2,1)}, bf16[64,512,256]{2,1,0:T(8,128)(2,1)S(1)}) custom-call(bf16[64,512,256]{2,1,0:T(8,128)(2,1)S(1)} %get-tuple-element.16.v_in, f32[2,64,256]{2,1,0:T(8,128)S(1)} %get-tuple-element.14.kv_row, s32[64]{0:T(128)} %pos_hbm.5, ...), custom_call_target="tpu_custom_call", output_to_operand_aliasing={{1}: (0, {}), {0}: (3, {})} | custom-call | flops 600000000 | bytes 13000000 | tf_op jit(solution)/shard_map/store_second/pallas_call | solution.py:349
  42.9 0.0 collective-permute-done.1.pair_own
  43.0 0.0 collective-permute-done.2.pair_other
  43.0 0.8 %final.1 = bf16[64,2048]{1,0:T(8,128)(2,1)} custom-call(f32[80,1024]{1,0:T(8,128)S(1)} %get-tuple-element.11.own, f32[80,1024]{1,0:T(8,128)S(1)} %collective-permute-done.other, f32[80,1024]{1,0:T(8,128)S(1)} %collective-permute-done.1.pair_own, f32[80,1024]{1,0:T(8,128)S(1)} %collective-permute-done.2.pair_other), custom_call_target="tpu_custom_call" | custom-call | flops 1000000 | bytes 1048576 | tf_op jit(solution)/shard_map/final/pallas_call | solution.py:355
Async XLA Ops:
  21.0 9.8 %collective-permute-start = (f32[80,1024]{1,0:T(8,128)S(1)}, f32[80,1024]{1,0:T(8,128)S(1)}, u32[]{:S(2)}, u32[]{:S(2)}) collective-permute-start(f32[80,1024]{1,0:T(8,128)S(1)} %get-tuple-element.11.own), channel_id=1, source_target_pairs={{0,2},{1,3},{2,0},{3,1},{4,6},{5,7},{6,4},{7,5}} | collective-permute-start | bytes 983048 | tf_op jit(solution)/shard_map/ppermute | solution.py:336
  21.1 21.8 %collective-permute-start.1 = (f32[80,1024]{1,0:T(8,128)S(1)}, f32[80,1024]{1,0:T(8,128)S(1)}, u32[]{:S(2)}, u32[]{:S(2)}) collective-permute-start(f32[80,1024]{1,0:T(8,128)S(1)} %get-tuple-element.11.own), channel_id=1, source_target_pairs={{0,1},{1,0},{2,3},{3,2},{4,5},{5,4},{6,7},{7,6}} | collective-permute-start | bytes 983048 | tf_op jit(solution)/shard_map/ppermute | solution.py:337
  30.8 12.2 %collective-permute-start.2 = (f32[80,1024]{1,0:T(8,128)S(1)}, f32[80,1024]{1,0:T(8,128)S(1)}, u32[]{:S(2)}, u32[]{:S(2)}) collective-permute-start(f32[80,1024]{1,0:T(8,128)S(1)} %collective-permute-done.other), channel_id=1, source_target_pairs={{0,1},{1,0},{2,3},{3,2},{4,5},{5,4},{6,7},{7,6}} | collective-permute-start | bytes 983048 | tf_op jit(solution)/shard_map/ppermute | solution.py:338

commit v5 on v4

--- a/solution.py
+++ b/solution.py
@@ -11,8 +11,7 @@
 F32, BF16 = jnp.float32, jnp.bfloat16
 NEG_FLOOR = -1e30
 GROUP = 8
-FEED = (1, 1, 2, 2, 2, 2, 2)
-LATE = 6
+FEED = (1, 1, 1, 2, 2, 2, 2)
 CHUNKS = ((0, 48), (48, 64))
 SPLIT = 48
 EARLY = 1
@@ -36,13 +35,15 @@
     peers = pair, across, far = 2 * x + 1 - c, 2 * (1 - x) + c, 2 * (1 - x) + 1 - c
     start = i * span
     barrier = pltpu.get_barrier_semaphore()
-    for peer in peers:
-        pl.semaphore_signal(barrier, inc=1, device_id={'sp': peer}, device_id_type=MESH)
+
+    own_cols = pl.ds(pl.multiple_of(c * wide, wide), wide)
+    other_cols = pl.ds(pl.multiple_of((1 - c) * wide, wide), wide)
 
     def fetch(kind, g):
         part = pl.ds(g * GROUP, GROUP)
         if kind == 'o':
-            return pltpu.make_async_copy(wo_hbm, wo, sem_w.at[2])
+            cols = other_cols if g == 0 else own_cols
+            return pltpu.make_async_copy(wo_hbm.at[:, cols], wo.at[:, cols], sem_w.at[2 if g == 0 else 3 + mine])
         if kind == 'k':
             return pltpu.make_async_copy(k_hbm.at[part], k_buf.at[part], sem_k.at[g])
         if g == groups - 1:
@@ -79,11 +80,12 @@
         q_part(h).start()
     for copy in scal:
         copy.start()
+    for peer in peers:
+        pl.semaphore_signal(barrier, inc=1, device_id={'sp': peer}, device_id_type=MESH)
     order = [('k', 0)]
     for g in range(1, groups):
         order += [('k', g), ('v', g - 1)]
     order += [('v', groups - 1), ('w', groups - 1)]
-    order.insert(2 * LATE, ('o', 0))
     started = []
 
     def begin(count):
@@ -147,6 +149,8 @@
         for j in range(GROUP):
             if g == groups - 1 and j == GROUP // 2:
                 fetch('w', g).wait()
+                fetch('o', 0).start()
+                fetch('o', 1).start()
             out.append(jnp.dot(probs[j], v_buf[base + j], preferred_element_type=F32) + extra[j] * kv_row[1, base + j:base + j + 1, :])
         acc[:, base:base + GROUP, :] = jnp.swapaxes(jnp.stack(out), 0, 1)
 
@@ -161,9 +165,6 @@
         if n < 3:
             return to(ml.at[k], ml_in.at[n, k], sems, (n, k), peers[n])
         return to(half, part3, sems, (n, k), pair)
-
-    own_cols = pl.ds(pl.multiple_of(c * wide, wide), wide)
-    other_cols = pl.ds(pl.multiple_of((1 - c) * wide, wide), wide)
 
     def col_of(v, h):
         lane = lax.broadcasted_iota(jnp.int32, v.shape, 1)
@@ -184,8 +185,6 @@
         inv = 1.0 / functools.reduce(jnp.add, [l * e for (_, l), e in zip(stats, scale)])
         scale = [e * inv for e in scale]
         cols = [[col_of(e, heads_of(i) + j) for e in scale] for j in range(2)]
-        if k == 0:
-            fetch('o', 0).wait()
         for q in range(3):
             for g in range(r0 // GROUP, r1 // GROUP):
                 give_acc(g, q).wait()
@@ -209,21 +208,23 @@
         blend(g, *held)
         held = following
         for k, (r0, r1) in enumerate(CHUNKS):
-            if r1 == (g + 1) * GROUP:
+            if r1 == (g + 2) * GROUP:
                 for n in (1, 2, 0):
                     give(n, k).start()
         for n in (1, 2, 0):
             give_acc(g, n).start()
     o = combine(0)
     early = CHUNKS[0][1]
+    fetch('o', 0).wait()
     half[...] = jnp.dot(o, wo[:, other_cols], preferred_element_type=F32)
     give(3, 0).start()
-    total[:early] = jnp.dot(o, wo[:, own_cols], preferred_element_type=F32)
+    last = combine(1)
+    fetch('o', 1).wait()
+    own = jnp.dot(jnp.concatenate([o, last], axis=0), wo[:, own_cols], preferred_element_type=F32)
+    total[early:rows] = own[early:]
+    total[rows:] = jnp.dot(last, wo[:, other_cols], preferred_element_type=F32)
     give(3, 0).wait()
-    total[:early] += part3[...]
-    o = combine(1)
-    total[early:rows] = jnp.dot(o, wo[:, own_cols], preferred_element_type=F32)
-    total[rows:] = jnp.dot(o, wo[:, other_cols], preferred_element_type=F32)
+    total[:early] = own[:early] + part3[...]
 
 
 def store(jobs, kv_row, pos_hbm, bufs, outs, pos, sem_p, sem_g, sem_w):
@@ -283,7 +284,7 @@
     store(jobs, kv_row, pos_hbm, (v_buf, v_buf), (v_out, v_out), *rest)
 
 
-def final(own, other, pair_own, pair_other, out):
+def final(own, other, pair_own, pair_other, att, out, sem):
     rows, wide = out.shape[0], own.shape[1]
     early = CHUNKS[0][1]
     c = lax.axis_index('sp') % 2
@@ -292,8 +293,14 @@
     a, b = slice(early, rows), slice(rows, 2 * rows - early)
     out[:early, own_cols] = (own[:early] + other[:early]).astype(BF16)
     out[:early, other_cols] = (pair_own[:early] + pair_other[:early]).astype(BF16)
+    first = pltpu.make_async_copy(out.at[:early], att.at[:early], sem.at[0])
+    first.start()
     out[early:, own_cols] = ((own[a] + pair_own[b]) + (other[a] + pair_other[b])).astype(BF16)
     out[early:, other_cols] = ((own[b] + pair_own[a]) + (other[b] + pair_other[a])).astype(BF16)
+    rest = pltpu.make_async_copy(out.at[early:], att.at[early:], sem.at[1])
+    rest.start()
+    first.wait()
+    rest.wait()
 
 
 def solution(mesh):
@@ -325,7 +332,7 @@
                             pltpu.VMEM((heads, rows, dim), F32), pltpu.VMEM((chunks, heads, 128), F32), pltpu.VMEM((3, chunks, heads, 128), F32),
                             pltpu.VMEM((3,) + pair, F32),
                             pltpu.VMEM((CHUNKS[0][1], wide), F32), pltpu.VMEM((CHUNKS[0][1], wide), F32),
-                            dma((3 + heads // 2,)), dma((2,)), dma((rows // GROUP,)), dma((rows // GROUP + 1,)), dma((2,)), dma((2,)),
+                            dma((4 + heads // 2,)), dma((2,)), dma((rows // GROUP,)), dma((rows // GROUP + 1,)), dma((2,)), dma((2,)),
                             dma((3, rows // GROUP)), dma((3, rows // GROUP)), dma((4, chunks)), dma((4, chunks))],
             compiler_params=pltpu.CompilerParams(collective_id=0, has_side_effects=True, vmem_limit_bytes=12 * 2 ** 20),
             cost_estimate=pl.CostEstimate(flops=10 ** 9, bytes_accessed=46 * 10 ** 6, transcendentals=0),
@@ -354,9 +361,10 @@
         )(vm(v_mid), vm(kv_row), hbm(write_pos), v_part)
         attn_out = pl.pallas_call(
             final,
-            out_shape=jax.ShapeDtypeStruct((rows, w_out.shape[1]), BF16),
+            out_shape=pltpu.HBM((rows, w_out.shape[1]), BF16),
             in_specs=[VMEM] * 4,
-            out_specs=VMEM,
+            out_specs=ANY,
+            scratch_shapes=[pltpu.VMEM((rows, w_out.shape[1]), BF16), dma((2,))],
             compiler_params=pltpu.CompilerParams(vmem_limit_bytes=4 * 2 ** 20),
             cost_estimate=pl.CostEstimate(flops=10 ** 6, bytes_accessed=2 ** 20, transcendentals=0),
             name='final',

time: 43.8 us -> 43.2 us (0.986)
  Pallas kernels: 33.3 us -> 32.6 us
    pallas_call x1, Pallas kernels: 20.3 us -> 19.7 us  [one_step(): pl.pallas_call(attend, out_shape=[pltpu.VMEM((2 * rows - CHUNKS[0][1], wi...]
where the time goes in v5:
time: 43.2 us; the launch traced here: 43 us
  Pallas kernels  32.6 us (75%)
  waiting for transfers between devices  9.37 us (22%)
  between operations  0.67 us (2%)
    pallas_call x1, Pallas kernels, one_step(): pl.pallas_call(attend, out_shape=[pltpu.VMEM((2 * rows - CHUNKS[0][1], wi...  19.7 us
    pallas_call x1, Pallas kernels, one_step(): pl.pallas_call(functools.partial(store_first, jobs=((0, 0, rows), (1, 0,...  9.9 us
    ppermute x1, waiting for transfers between devices, one_step(): other = lax.ppermute(total, 'sp', across)  9.36 us
    pallas_call x1, Pallas kernels, one_step(): pl.pallas_call(functools.partial(store_second, jobs=((1, SPLIT, rows),)),...  2.28 us
  transfers between devices with their start and end apart: 3, of which 1 were waited for; matrix products, arithmetic and copies ran while one was open for 0% of the time, Pallas kernels for 28%

profile of v5, /device:TPU:0, one launch (start us, length us, event | category | flops | bytes accessed | tf_op | source)
XLA Modules:
  0.0 43.0 jit_solution(11469091334791367258)
XLA Ops:
  0.6 19.7 %attend.1 = (f32[80,1024]{1,0:T(8,128)S(1)}, bf16[64,512,256]{2,1,0:T(8,128)(2,1)S(1)}, bf16[64,512,256]{2,1,0:T(8,128)(2,1)S(1)}, f32[2,64,256]{2,1,0:T(8,128)S(1)}) custom-call(bf16[64,2048]{1,0:T(8,128)(2,1)} %hid_hbm.1, bf16[2048,2048]{1,0:T(8,128)(2,1)} %wq_hbm.1, bf16[2048,256]{1,0:T(8,128)(2,1)} %wk_hbm.1, bf16[2048,256]{1,0:T(8,128)(2,1)} %wv_hbm.1, ...), custom_call_target="tpu_custom_call" | custom-call | flops 1000000000 | bytes 46000000 | tf_op jit(solution)/shard_map/attend/pallas_call | solution.py:322
  20.3 0.3 collective-permute-start
  20.6 0.1 collective-permute-start.1
  20.7 9.4 %collective-permute-done.other = f32[80,1024]{1,0:T(8,128)S(1)} collective-permute-done((f32[80,1024]{1,0:T(8,128)S(1)}, f32[80,1024]{1,0:T(8,128)S(1)}, u32[]{:S(2)}, u32[]{:S(2)}) %collective-permute-start) | collective-permute-done | bytes 327712 | tf_op jit(solution)/shard_map/ppermute | solution.py:343
  30.1 0.0 collective-permute-start.2
  30.1 9.9 %store_first.1 = (bf16[64,512,256]{2,1,0:T(8,128)(2,1)}, bf16[64,512,256]{2,1,0:T(8,128)(2,1)}, bf16[64,512,256]{2,1,0:T(8,128)(2,1)S(1)}, bf16[64,512,256]{2,1,0:T(8,128)(2,1)S(1)}) custom-call(bf16[64,512,256]{2,1,0:T(8,128)(2,1)S(1)} %get-tuple-element.12.k_in, ...), custom_call_target="tpu_custom_call", output_to_operand_aliasing={{2}: (0, {}), {3}: (1, {})} | custom-call | flops 1000000000 | bytes 21000000 | tf_op jit(solution)/shard_map/store_first/pallas_call | solution.py:350
  40.0 2.3 %store_second.1 = (bf16[64,512,256]{2,1,0:T(8,128)(2,1)}, bf16[64,512,256]{2,1,0:T(8,128)(2,1)S(1)}) custom-call(bf16[64,512,256]{2,1,0:T(8,128)(2,1)S(1)} %get-tuple-element.16.v_in, f32[2,64,256]{2,1,0:T(8,128)S(1)} %get-tuple-element.14.kv_row, s32[64]{0:T(128)} %pos_hbm.5, ...), custom_call_target="tpu_custom_call", output_to_operand_aliasing={{1}: (0, {}), {0}: (3, {})} | custom-call | flops 600000000 | bytes 13000000 | tf_op jit(solution)/shard_map/store_second/pallas_call | solution.py:356
  42.3 0.0 collective-permute-done.1.pair_own
  42.3 0.0 collective-permute-done.2.pair_other
  42.3 0.8 %final.1 = bf16[64,2048]{1,0:T(8,128)(2,1)} custom-call(f32[80,1024]{1,0:T(8,128)S(1)} %get-tuple-element.11.own, f32[80,1024]{1,0:T(8,128)S(1)} %collective-permute-done.other, f32[80,1024]{1,0:T(8,128)S(1)} %collective-permute-done.1.pair_own, f32[80,1024]{1,0:T(8,128)S(1)} %collective-permute-done.2.pair_other), custom_call_target="tpu_custom_call" | custom-call | flops 1000000 | bytes 1048576 | tf_op jit(solution)/shard_map/final/pallas_call | solution.py:362
Async XLA Ops:
  20.3 9.7 %collective-permute-start = (f32[80,1024]{1,0:T(8,128)S(1)}, f32[80,1024]{1,0:T(8,128)S(1)}, u32[]{:S(2)}, u32[]{:S(2)}) collective-permute-start(f32[80,1024]{1,0:T(8,128)S(1)} %get-tuple-element.11.own), channel_id=1, source_target_pairs={{0,2},{1,3},{2,0},{3,1},{4,6},{5,7},{6,4},{7,5}} | collective-permute-start | bytes 983048 | tf_op jit(solution)/shard_map/ppermute | solution.py:343
  20.6 21.6 %collective-permute-start.1 = (f32[80,1024]{1,0:T(8,128)S(1)}, f32[80,1024]{1,0:T(8,128)S(1)}, u32[]{:S(2)}, u32[]{:S(2)}) collective-permute-start(f32[80,1024]{1,0:T(8,128)S(1)} %get-tuple-element.11.own), channel_id=1, source_target_pairs={{0,1},{1,0},{2,3},{3,2},{4,5},{5,4},{6,7},{7,6}} | collective-permute-start | bytes 983048 | tf_op jit(solution)/shard_map/ppermute | solution.py:344
  30.1 12.2 %collective-permute-start.2 = (f32[80,1024]{1,0:T(8,128)S(1)}, f32[80,1024]{1,0:T(8,128)S(1)}, u32[]{:S(2)}, u32[]{:S(2)}) collective-permute-start(f32[80,1024]{1,0:T(8,128)S(1)} %collective-permute-done.other), channel_id=1, source_target_pairs={{0,1},{1,0},{2,3},{3,2},{4,5},{5,4},{6,7},{7,6}} | collective-permute-start | bytes 983048 | tf_op jit(solution)/shard_map/ppermute | solution.py:345

commit v6 on v5

--- a/solution.py
+++ b/solution.py
@@ -13,7 +13,8 @@
 GROUP = 8
 FEED = (1, 1, 1, 2, 2, 2, 2)
 CHUNKS = ((0, 48), (48, 64))
-SPLIT = 48
+SPLIT = 56
+LAST = 2
 EARLY = 1
 ANY = pl.BlockSpec(memory_space=pl.ANY)
 VMEM = pl.BlockSpec(memory_space=pltpu.VMEM)
@@ -47,7 +48,7 @@
         if kind == 'k':
             return pltpu.make_async_copy(k_hbm.at[part], k_buf.at[part], sem_k.at[g])
         if g == groups - 1:
-            part = pl.ds(g * GROUP + (kind == 'w') * GROUP // 2, GROUP // 2)
+            part = pl.ds(g * GROUP + (kind == 'w') * (GROUP - LAST), LAST if kind == 'w' else GROUP - LAST)
         return pltpu.make_async_copy(v_hbm.at[part], v_buf.at[part], sem_v.at[g + (kind == 'w')])
 
     def q_part(h):
@@ -147,9 +148,9 @@
         base = g * GROUP
         out = []
         for j in range(GROUP):
-            if g == groups - 1 and j == GROUP // 2:
+            if g == groups - 1 and j == GROUP - LAST:
+                fetch('o', 0).start()
                 fetch('w', g).wait()
-                fetch('o', 0).start()
                 fetch('o', 1).start()
             out.append(jnp.dot(probs[j], v_buf[base + j], preferred_element_type=F32) + extra[j] * kv_row[1, base + j:base + j + 1, :])
         acc[:, base:base + GROUP, :] = jnp.swapaxes(jnp.stack(out), 0, 1)
@@ -185,17 +186,12 @@
         inv = 1.0 / functools.reduce(jnp.add, [l * e for (_, l), e in zip(stats, scale)])
         scale = [e * inv for e in scale]
         cols = [[col_of(e, heads_of(i) + j) for e in scale] for j in range(2)]
-        for q in range(3):
+        o = [acc[heads_of(i) + j, rs] * cols[j][0] for j in range(2)]
+        for q in (0, 1, 2):
             for g in range(r0 // GROUP, r1 // GROUP):
                 give_acc(g, q).wait()
-        o = []
-        for j in range(2):
-            part = acc[heads_of(i) + j, rs] * cols[j][0]
-            for q in range(3):
-                part += parts[q, j, rs] * cols[j][q + 1]
-            o.append(part.astype(BF16))
-        o = jnp.concatenate(o, axis=1)
-        return o
+            o = [o[j] + parts[q, j, rs] * cols[j][q + 1] for j in range(2)]
+        return jnp.concatenate([part.astype(BF16) for part in o], axis=1)
 
     fetch('k', 0).wait()
     held = score(0)
@@ -266,6 +262,8 @@
     for cut in later:
         patch(*cut)
         put(*cut).start()
+    for r in range(jobs[-1][2], bufs[1].shape[0], GROUP):
+        patch(1, r)
     for cut in early:
         put(*cut).wait()
         patch(*cut)
@@ -280,8 +278,13 @@
     store(jobs, kv_row, pos_hbm, (k_buf, v_buf), (k_out, v_out), *rest)
 
 
-def store_second(v_in, kv_row, pos_hbm, v_old, v_out, v_buf, *rest, jobs):
-    store(jobs, kv_row, pos_hbm, (v_buf, v_buf), (v_out, v_out), *rest)
+def store_second(v_in, v_old, v_out, v_buf, sem):
+    copies = [pltpu.make_async_copy(v_buf.at[pl.ds(r, GROUP)], v_out.at[pl.ds(r, GROUP)], sem.at[n])
+              for n, r in enumerate(range(SPLIT, v_buf.shape[0], GROUP))]
+    for copy in copies:
+        copy.start()
+    for copy in copies:
+        copy.wait()
 
 
 def final(own, other, pair_own, pair_other, att, out, sem):
@@ -354,11 +357,12 @@
             cost_estimate=pl.CostEstimate(flops=10 ** 9, bytes_accessed=21 * 10 ** 6, transcendentals=0), **common,
         )(vm(k_mid), vm(v_mid), vm(kv_row), hbm(write_pos))
         v_new, _ = pl.pallas_call(
-            functools.partial(store_second, jobs=((1, SPLIT, rows),)),
-            out_shape=[full, held], in_specs=[VMEM, VMEM, ANY, ANY], out_specs=[ANY, VMEM],
-            input_output_aliases={0: 1, 3: 0}, name='store_second',
-            cost_estimate=pl.CostEstimate(flops=6 * 10 ** 8, bytes_accessed=13 * 10 ** 6, transcendentals=0), **common,
-        )(vm(v_mid), vm(kv_row), hbm(write_pos), v_part)
+            store_second,
+            out_shape=[full, held], in_specs=[VMEM, ANY], out_specs=[ANY, VMEM],
+            input_output_aliases={0: 1, 1: 0}, name='store_second', scratch_shapes=[dma(((rows - SPLIT) // GROUP,))],
+            compiler_params=common['compiler_params'],
+            cost_estimate=pl.CostEstimate(flops=6 * 10 ** 8, bytes_accessed=13 * 10 ** 6, transcendentals=0),
+        )(vm(v_mid), v_part)
         attn_out = pl.pallas_call(
             final,
             out_shape=pltpu.HBM((rows, w_out.shape[1]), BF16),

time: 43.2 us -> 42.8 us (level)
    pallas_call x1, Pallas kernels: 2.28 us -> 1.33 us  [one_step(): pl.pallas_call(store_second, out_shape=[full, held], in_specs=[VMEM, ANY]...]
    pallas_call x1, Pallas kernels: 9.9 us -> 10.5 us  [one_step(): pl.pallas_call(functools.partial(store_first, jobs=((0, 0, rows), (1, 0,...]
where the time goes in v6:
time: 42.8 us; the launch traced here: 42.7 us
  Pallas kernels  32.3 us (75%)
  waiting for transfers between devices  9.59 us (22%)
  between operations  0.68 us (2%)
    pallas_call x1, Pallas kernels, one_step(): pl.pallas_call(attend, out_shape=[pltpu.VMEM((2 * rows - CHUNKS[0][1], wi...  19.7 us
    pallas_call x1, Pallas kernels, one_step(): pl.pallas_call(functools.partial(store_first, jobs=((0, 0, rows), (1, 0,...  10.5 us
    ppermute x1, waiting for transfers between devices, one_step(): other = lax.ppermute(total, 'sp', across)  9.58 us
    pallas_call x1, Pallas kernels, one_step(): pl.pallas_call(store_second, out_shape=[full, held], in_specs=[VMEM, ANY]...  1.33 us
  transfers between devices with their start and end apart: 3, of which 1 were waited for; matrix products, arithmetic and copies ran while one was open for 0% of the time, Pallas kernels for 28%

profile of v6, /device:TPU:0, one launch (start us, length us, event | category | flops | bytes accessed | tf_op | source)
XLA Modules:
  0.0 42.7 jit_solution(6431911500255677054)
XLA Ops:
  0.6 19.7 %attend.1 = (f32[80,1024]{1,0:T(8,128)S(1)}, bf16[64,512,256]{2,1,0:T(8,128)(2,1)S(1)}, bf16[64,512,256]{2,1,0:T(8,128)(2,1)S(1)}, f32[2,64,256]{2,1,0:T(8,128)S(1)}) custom-call(bf16[64,2048]{1,0:T(8,128)(2,1)} %hid_hbm.1, bf16[2048,2048]{1,0:T(8,128)(2,1)} %wq_hbm.1, bf16[2048,256]{1,0:T(8,128)(2,1)} %wk_hbm.1, bf16[2048,256]{1,0:T(8,128)(2,1)} %wv_hbm.1, ...), custom_call_target="tpu_custom_call" | custom-call | flops 1000000000 | bytes 46000000 | tf_op jit(solution)/shard_map/attend/pallas_call | solution.py:325
  20.3 0.0 collective-permute-start
  20.4 0.1 collective-permute-start.1
  20.5 9.6 %collective-permute-done.other = f32[80,1024]{1,0:T(8,128)S(1)} collective-permute-done((f32[80,1024]{1,0:T(8,128)S(1)}, f32[80,1024]{1,0:T(8,128)S(1)}, u32[]{:S(2)}, u32[]{:S(2)}) %collective-permute-start) | collective-permute-done | bytes 327712 | tf_op jit(solution)/shard_map/ppermute | solution.py:346
  30.1 0.0 collective-permute-start.2
  30.1 10.5 %store_first.1 = (bf16[64,512,256]{2,1,0:T(8,128)(2,1)}, bf16[64,512,256]{2,1,0:T(8,128)(2,1)}, bf16[64,512,256]{2,1,0:T(8,128)(2,1)S(1)}, bf16[64,512,256]{2,1,0:T(8,128)(2,1)S(1)}) custom-call(bf16[64,512,256]{2,1,0:T(8,128)(2,1)S(1)} %get-tuple-element.12.k_in, ...), custom_call_target="tpu_custom_call", output_to_operand_aliasing={{2}: (0, {}), {3}: (1, {})} | custom-call | flops 1000000000 | bytes 21000000 | tf_op jit(solution)/shard_map/store_first/pallas_call | solution.py:353
  40.6 1.3 %store_second.1 = (bf16[64,512,256]{2,1,0:T(8,128)(2,1)}, bf16[64,512,256]{2,1,0:T(8,128)(2,1)S(1)}) custom-call(bf16[64,512,256]{2,1,0:T(8,128)(2,1)S(1)} %get-tuple-element.16.v_in, bf16[64,512,256]{2,1,0:T(8,128)(2,1)} %get-tuple-element.17.v_old), custom_call_target="tpu_custom_call", output_to_operand_aliasing={{1}: (0, {}), {0}: (1, {})} | custom-call | flops 600000000 | bytes 13000000 | tf_op jit(solution)/shard_map/store_second/pallas_call | solution.py:359
  42.0 0.0 collective-permute-done.1.pair_own
  42.0 0.0 collective-permute-done.2.pair_other
  42.0 0.8 %final.1 = bf16[64,2048]{1,0:T(8,128)(2,1)} custom-call(f32[80,1024]{1,0:T(8,128)S(1)} %get-tuple-element.11.own, f32[80,1024]{1,0:T(8,128)S(1)} %collective-permute-done.other, f32[80,1024]{1,0:T(8,128)S(1)} %collective-permute-done.1.pair_own, f32[80,1024]{1,0:T(8,128)S(1)} %collective-permute-done.2.pair_other), custom_call_target="tpu_custom_call" | custom-call | flops 1000000 | bytes 1048576 | tf_op jit(solution)/shard_map/final/pallas_call | solution.py:366
Async XLA Ops:
  20.3 9.7 %collective-permute-start = (f32[80,1024]{1,0:T(8,128)S(1)}, f32[80,1024]{1,0:T(8,128)S(1)}, u32[]{:S(2)}, u32[]{:S(2)}) collective-permute-start(f32[80,1024]{1,0:T(8,128)S(1)} %get-tuple-element.11.own), channel_id=1, source_target_pairs={{0,2},{1,3},{2,0},{3,1},{4,6},{5,7},{6,4},{7,5}} | collective-permute-start | bytes 983048 | tf_op jit(solution)/shard_map/ppermute | solution.py:346
  20.4 21.6 %collective-permute-start.1 = (f32[80,1024]{1,0:T(8,128)S(1)}, f32[80,1024]{1,0:T(8,128)S(1)}, u32[]{:S(2)}, u32[]{:S(2)}) collective-permute-start(f32[80,1024]{1,0:T(8,128)S(1)} %get-tuple-element.11.own), channel_id=1, source_target_pairs={{0,1},{1,0},{2,3},{3,2},{4,5},{5,4},{6,7},{7,6}} | collective-permute-start | bytes 983048 | tf_op jit(solution)/shard_map/ppermute | solution.py:347
  30.1 11.9 %collective-permute-start.2 = (f32[80,1024]{1,0:T(8,128)S(1)}, f32[80,1024]{1,0:T(8,128)S(1)}, u32[]{:S(2)}, u32[]{:S(2)}) collective-permute-start(f32[80,1024]{1,0:T(8,128)S(1)} %collective-permute-done.other), channel_id=1, source_target_pairs={{0,1},{1,0},{2,3},{3,2},{4,5},{5,4},{6,7},{7,6}} | collective-permute-start | bytes 983048 | tf_op jit(solution)/shard_map/ppermute | solution.py:348

commit v7 on v6

--- a/solution.py
+++ b/solution.py
@@ -9,7 +9,7 @@
 
 
 F32, BF16 = jnp.float32, jnp.bfloat16
-NEG_FLOOR = -1e30
+NEG_FLOOR = float(jnp.finfo(jnp.float32).min)
 GROUP = 8
 FEED = (1, 1, 1, 2, 2, 2, 2)
 CHUNKS = ((0, 48), (48, 64))
@@ -214,13 +214,13 @@
     fetch('o', 0).wait()
     half[...] = jnp.dot(o, wo[:, other_cols], preferred_element_type=F32)
     give(3, 0).start()
-    last = combine(1)
     fetch('o', 1).wait()
-    own = jnp.dot(jnp.concatenate([o, last], axis=0), wo[:, own_cols], preferred_element_type=F32)
-    total[early:rows] = own[early:]
-    total[rows:] = jnp.dot(last, wo[:, other_cols], preferred_element_type=F32)
+    total[:early] = jnp.dot(o, wo[:, own_cols], preferred_element_type=F32)
+    o = combine(1)
+    total[early:rows] = jnp.dot(o, wo[:, own_cols], preferred_element_type=F32)
+    total[rows:] = jnp.dot(o, wo[:, other_cols], preferred_element_type=F32)
     give(3, 0).wait()
-    total[:early] = own[:early] + part3[...]
+    total[:early] += part3[...]
 
 
 def store(jobs, kv_row, pos_hbm, bufs, outs, pos, sem_p, sem_g, sem_w):

time: 42.8 us -> 42.8 us (level)
  no operation moved by 1% of the time
where the time goes in v7:
time: 42.8 us; the launch traced here: 42.7 us
  Pallas kernels  32.3 us (75%)
  waiting for transfers between devices  9.59 us (22%)
  between operations  0.68 us (2%)
    pallas_call x1, Pallas kernels, one_step(): pl.pallas_call(attend, out_shape=[pltpu.VMEM((2 * rows - CHUNKS[0][1], wi...  19.6 us
    pallas_call x1, Pallas kernels, one_step(): pl.pallas_call(functools.partial(store_first, jobs=((0, 0, rows), (1, 0,...  10.5 us
    ppermute x1, waiting for transfers between devices, one_step(): other = lax.ppermute(total, 'sp', across)  9.58 us
    pallas_call x1, Pallas kernels, one_step(): pl.pallas_call(store_second, out_shape=[full, held], in_specs=[VMEM, ANY]...  1.33 us
  transfers between devices with their start and end apart: 3, of which 1 were waited for; matrix products, arithmetic and copies ran while one was open for 0% of the time, Pallas kernels for 28%

profile of v7, /device:TPU:0, one launch (start us, length us, event | category | flops | bytes accessed | tf_op | source)
XLA Modules:
  0.0 42.7 jit_solution(17126783730369244109)
XLA Ops:
  0.6 19.6 %attend.1 = (f32[80,1024]{1,0:T(8,128)S(1)}, bf16[64,512,256]{2,1,0:T(8,128)(2,1)S(1)}, bf16[64,512,256]{2,1,0:T(8,128)(2,1)S(1)}, f32[2,64,256]{2,1,0:T(8,128)S(1)}) custom-call(bf16[64,2048]{1,0:T(8,128)(2,1)} %hid_hbm.1, bf16[2048,2048]{1,0:T(8,128)(2,1)} %wq_hbm.1, bf16[2048,256]{1,0:T(8,128)(2,1)} %wk_hbm.1, bf16[2048,256]{1,0:T(8,128)(2,1)} %wv_hbm.1, ...), custom_call_target="tpu_custom_call" | custom-call | flops 1000000000 | bytes 46000000 | tf_op jit(solution)/shard_map/attend/pallas_call | solution.py:325
  20.3 0.0 collective-permute-start
  20.3 0.1 collective-permute-start.1
  20.4 9.6 %collective-permute-done.other = f32[80,1024]{1,0:T(8,128)S(1)} collective-permute-done((f32[80,1024]{1,0:T(8,128)S(1)}, f32[80,1024]{1,0:T(8,128)S(1)}, u32[]{:S(2)}, u32[]{:S(2)}) %collective-permute-start) | collective-permute-done | bytes 327712 | tf_op jit(solution)/shard_map/ppermute | solution.py:346
  30.0 0.0 collective-permute-start.2
  30.0 10.5 %store_first.1 = (bf16[64,512,256]{2,1,0:T(8,128)(2,1)}, bf16[64,512,256]{2,1,0:T(8,128)(2,1)}, bf16[64,512,256]{2,1,0:T(8,128)(2,1)S(1)}, bf16[64,512,256]{2,1,0:T(8,128)(2,1)S(1)}) custom-call(bf16[64,512,256]{2,1,0:T(8,128)(2,1)S(1)} %get-tuple-element.12.k_in, ...), custom_call_target="tpu_custom_call", output_to_operand_aliasing={{2}: (0, {}), {3}: (1, {})} | custom-call | flops 1000000000 | bytes 21000000 | tf_op jit(solution)/shard_map/store_first/pallas_call | solution.py:353
  40.6 1.3 %store_second.1 = (bf16[64,512,256]{2,1,0:T(8,128)(2,1)}, bf16[64,512,256]{2,1,0:T(8,128)(2,1)S(1)}) custom-call(bf16[64,512,256]{2,1,0:T(8,128)(2,1)S(1)} %get-tuple-element.16.v_in, bf16[64,512,256]{2,1,0:T(8,128)(2,1)} %get-tuple-element.17.v_old), custom_call_target="tpu_custom_call", output_to_operand_aliasing={{1}: (0, {}), {0}: (1, {})} | custom-call | flops 600000000 | bytes 13000000 | tf_op jit(solution)/shard_map/store_second/pallas_call | solution.py:359
  41.9 0.0 collective-permute-done.1.pair_own
  41.9 0.0 collective-permute-done.2.pair_other
  41.9 0.8 %final.1 = bf16[64,2048]{1,0:T(8,128)(2,1)} custom-call(f32[80,1024]{1,0:T(8,128)S(1)} %get-tuple-element.11.own, f32[80,1024]{1,0:T(8,128)S(1)} %collective-permute-done.other, f32[80,1024]{1,0:T(8,128)S(1)} %collective-permute-done.1.pair_own, f32[80,1024]{1,0:T(8,128)S(1)} %collective-permute-done.2.pair_other), custom_call_target="tpu_custom_call" | custom-call | flops 1000000 | bytes 1048576 | tf_op jit(solution)/shard_map/final/pallas_call | solution.py:366
Async XLA Ops:
  20.3 9.7 %collective-permute-start = (f32[80,1024]{1,0:T(8,128)S(1)}, f32[80,1024]{1,0:T(8,128)S(1)}, u32[]{:S(2)}, u32[]{:S(2)}) collective-permute-start(f32[80,1024]{1,0:T(8,128)S(1)} %get-tuple-element.11.own), channel_id=1, source_target_pairs={{0,2},{1,3},{2,0},{3,1},{4,6},{5,7},{6,4},{7,5}} | collective-permute-start | bytes 983048 | tf_op jit(solution)/shard_map/ppermute | solution.py:346
  20.3 21.6 %collective-permute-start.1 = (f32[80,1024]{1,0:T(8,128)S(1)}, f32[80,1024]{1,0:T(8,128)S(1)}, u32[]{:S(2)}, u32[]{:S(2)}) collective-permute-start(f32[80,1024]{1,0:T(8,128)S(1)} %get-tuple-element.11.own), channel_id=1, source_target_pairs={{0,1},{1,0},{2,3},{3,2},{4,5},{5,4},{6,7},{7,6}} | collective-permute-start | bytes 983048 | tf_op jit(solution)/shard_map/ppermute | solution.py:347
  30.0 11.9 %collective-permute-start.2 = (f32[80,1024]{1,0:T(8,128)S(1)}, f32[80,1024]{1,0:T(8,128)S(1)}, u32[]{:S(2)}, u32[]{:S(2)}) collective-permute-start(f32[80,1024]{1,0:T(8,128)S(1)} %collective-permute-done.other), channel_id=1, source_target_pairs={{0,1},{1,0},{2,3},{3,2},{4,5},{5,4},{6,7},{7,6}} | collective-permute-start | bytes 983048 | tf_op jit(solution)/shard_map/ppermute | solution.py:348
